TPU v7x, 768 devices: a whole 4x8x12 slice. The times are simulated.
768 devices in a mesh: gz: 16 (over y, x_lo), gy: 48 (over z, x_hi, core).
Axes of the slice: x: 4 (x_hi: 2, x_lo: 2; x = x_hi * 2 + x_lo), y: 8, z: 12, core: 2. Of those that a mesh axis runs over, the one named last changes fastest.
Arguments:
- velocity: float32 [3, 128, 768, 768], P(None, 'gz', 'gy'), may hold values from -6 to 6
- forces: bfloat16 [24576, 3, 128], P(('gz', 'gy')), may hold values from -6 to 6
- kernels: bfloat16 [24576, 128, 256], P(('gz', 'gy')), may hold values from -0.5 to 0.5
- owners: int32 [24576, 1], P(('gz', 'gy')), may hold values from 0 to 47; in each aligned block of 32 rows (0 to 31, 32 to 63, ...) at most 2 rows name the same one
- blocks: int32 [24576], P(('gz', 'gy')), may hold values from 0 to 383
- counts: int32 [768], P(('gz', 'gy')), may hold values from 16 to 32, as said below
Outputs:
- velocity_next: float32 [3, 128, 768, 768], P(None, 'gz', 'gy')
- patch_velocity: float32 [24576, 3, 128], P(('gz', 'gy'))
Inputs may be any that keep to these rules, and one draw needn't show every extreme that they name: `owners`: owners are gy indices in the holder's own row along gz; among the 32 patches of one device at most 2 share an owner, and some owner has exactly 2. `blocks`: A cell block index within the owner's part of the grid. `counts`: live patches come first in a device's slots; some device has all 32 live.
All inputs are finite; a program needn't handle non-finite values.
Results may differ from a plain program's by a relative error of at most 0.0027.
Values may be sent and summed in bfloat16 or wider, within the bound.
No kernel may reach another device: no remote copies, remote signals or barrier semaphores. Data moves between devices by JAX's collectives and lax.ppermute only.
A program may use at most 32 MiB of HBM per device.

v0:
```python
import jax
import jax.numpy as jnp
from jax import lax
from jax.sharding import PartitionSpec as P

time_step = 0.25
viscosity = 0.5


def padded_2(block, sides, width):
    for axis, dim in sides:
        count = lax.axis_size(axis)
        forward = [(i, i + 1) for i in range(count - 1)]
        backward = [(target, source) for source, target in forward]
        low = lax.ppermute(
            lax.slice_in_dim(block, block.shape[dim] - width, None, axis=dim), axis, forward
        )
        high = lax.ppermute(lax.slice_in_dim(block, 0, width, axis=dim), axis, backward)
        block = jnp.concatenate([low, block, high], axis=dim)
    return block


def local(velocity, forces, kernels, owners, blocks, counts):
    width_gy = lax.axis_size("gy")
    slots = forces.shape[0]
    cells = kernels.shape[2]
    planes, rows, xcells = (velocity.shape[1], velocity.shape[2], velocity.shape[3])
    nblock = planes * rows * (xcells // cells)
    room = max(2, (2 * slots + width_gy - 1) // width_gy)
    live = (jnp.arange(slots, dtype=jnp.int32) < counts[0]).astype(jnp.float32)
    product = jnp.einsum("pcq,pqb->pcb", forces, kernels, preferred_element_type=jnp.float32)
    contribution = (product * live[:, None, None]).astype(jnp.bfloat16)
    owner = owners[:, 0]
    onehot = (owner[:, None] == jnp.arange(width_gy, dtype=jnp.int32)[None, :]).astype(jnp.int32)
    rank = jnp.sum((jnp.cumsum(onehot, 0) - onehot) * onehot, 1)
    slot = owner * room + rank
    send_blocks = jnp.zeros((width_gy * room, 3, cells), jnp.bfloat16).at[slot].set(contribution)
    send_ids = jnp.zeros((width_gy * room,), jnp.int32).at[slot].set(blocks)
    got_blocks, got_ids = (
        lax.all_to_all(send_blocks, "gy", split_axis=0, concat_axis=0, tiled=True),
        lax.all_to_all(send_ids, "gy", split_axis=0, concat_axis=0, tiled=True),
    )
    force = jax.ops.segment_sum(got_blocks.astype(jnp.float32), got_ids, num_segments=nblock)
    force_grid = force.transpose(1, 0, 2).reshape(3, planes, rows, xcells)
    padded = padded_2(velocity, (("gz", 1), ("gy", 2)), 1)
    z_up = padded[:, 2:, 1:-1, :]
    z_down = padded[:, :-2, 1:-1, :]
    y_up = padded[:, 1:-1, 2:, :]
    y_down = padded[:, 1:-1, :-2, :]
    edge = jnp.zeros_like(velocity[..., :1])
    x_up = jnp.concatenate([velocity[..., 1:], edge], -1)
    x_down = jnp.concatenate([edge, velocity[..., :-1]], -1)
    lap = x_up + x_down + y_up + y_down + z_up + z_down - 6.0 * velocity
    adv = (
        velocity[0:1] * (x_up - x_down) * 0.5
        + velocity[1:2] * (y_up - y_down) * 0.5
        + velocity[2:3] * (z_up - z_down) * 0.5
    )
    fresh = velocity + time_step * (viscosity * lap - adv + force_grid)
    cell_blocks = fresh.reshape(3, nblock, cells)
    picked = jnp.take(cell_blocks, got_ids, axis=1).transpose(1, 0, 2).astype(jnp.bfloat16)
    back = lax.all_to_all(picked, "gy", split_axis=0, concat_axis=0, tiled=True)
    mine_blocks = back[slot]
    sampled = jnp.einsum("pcb,pqb->pcq", mine_blocks, kernels, preferred_element_type=jnp.float32)
    return (fresh, sampled * live[:, None, None])


def solution(mesh):
    return jax.shard_map(
        local,
        mesh=mesh,
        in_specs=(
            P(None, "gz", "gy", None),
            P(("gz", "gy"), None, None),
            P(("gz", "gy"), None, None),
            P(("gz", "gy"), None),
            P(("gz", "gy")),
            P(("gz", "gy")),
        ),
        out_specs=(P(None, "gz", "gy", None), P(("gz", "gy"), None, None)),
        check_vma=False,
    )
```

profile of v0, /device:TPU:1, one launch (start us, length us, event | category | flops | bytes accessed | tf_op | source)
XLA Modules:
  0.0 131.5 jit_solution(17951009542429100085)
XLA Ops:
  0.6 0.9 fusion.2
  1.6 0.8 select_reduce_fusion
  3.1 0.8 scatter_custom_fusion
  3.9 0.7 all_to_all.14
  4.6 19.4 %all-to-all-start = ((s32[48,2,1]{1,2,0:T(1,128)}), s32[48,2,1]{1,2,0:T(1,128)S(1)}, u32[]{:S(2)}, u32[]{:S(2)}) async-start(s32[48,2,1]{1,2,0:T(1,128)} %bitcast.6), calls=%async_computation | async-start | bytes 49152 | tf_op jit(solution)/shard_map/all_to_all | solution.py:41
  24.1 1.7 %fusion.9 = (f32[3,1,16,768]{3,2,1,0:T(8,128)}, f32[3,1,16,768]{3,2,1,0:T(8,128)}) fusion(f32[3,8,16,768]{3,2,1,0:T(8,128)} %param.6), kind=kLoop, calls=%fused_computation.38 | loop fusion | bytes 589824 | tf_op jit(solution)/shard_map/slice | solution.py:18
  25.8 1.3 collective-permute-start.1
  27.1 4.7 %collective-permute-start = (f32[3,1,16,768]{3,2,1,0:T(8,128)}, f32[3,1,16,768]{3,2,1,0:T(8,128)}, u32[]{:S(2)}, u32[]{:S(2)}) collective-permute-start(f32[3,1,16,768]{3,2,1,0:T(8,128)} %get-tuple-element.18), channel_id=1, source_target_pairs={{0,48},{48,96},{96,144},{144,192},{192,240},{240,288},{288,336},{3... | collective-permute-start | bytes 442376 | tf_op jit(solution)/shard_map/ppermute | solution.py:15
  31.7 3.5 %fusion.8 = (f32[3,8,16,767]{3,2,1,0:T(8,128)}, f32[3,8,16,767]{3,2,1,0:T(8,128)}) fusion(f32[3,8,16,768]{3,2,1,0:T(8,128)} %param.6), kind=kLoop, calls=%fused_computation.37 | loop fusion | bytes 4712448 | tf_op jit(solution)/shard_map/slice | solution.py:51
  36.6 1.1 slice_bitcast_fusion.2
  37.6 0.7 broadcast_in_dim.34
  38.4 4.2 %scatter_fusion = bf16[96,3,256]{2,1,0:T(4,128)(2,1)} fusion(bf16[96,3,256]{2,1,0:T(4,128)(2,1)} %broadcast_in_dim.34, s32[32]{0:T(128)S(1)} %fusion.3, bf16[32,3,256]{2,1,0:T(4,128)(2,1)S(1)} %fusion), kind=kCustom, calls=%fused_computation.3 | custom fusion | bytes 147584 | tf_op jit(solution)/shard_map/scatter | solution.py:37
  42.6 13.0 %all-to-all-start.1 = ((bf16[96,3,256]{2,1,0:T(4,128)(2,1)}), bf16[96,3,256]{2,1,0:T(4,128)(2,1)S(1)}, u32[]{:S(2)}, u32[]{:S(2)}) async-start(bf16[96,3,256]{2,1,0:T(4,128)(2,1)} %scatter_fusion), calls=%async_computation.1 | async-start | bytes 393216 | tf_op jit(solution)/shard_map/all_to_all | solution.py:40
  57.1 0.9 constant_dynamic-update-slice_fusion.2
  58.1 0.9 constant_dynamic-update-slice_fusion
  59.1 1.1 copy-done.2
  60.2 0.8 fusion.7
  61.0 2.2 %collective-permute-start.2 = (f32[3,10,1,768]{3,2,1,0:T(1,128)}, f32[3,10,1,768]{3,2,1,0:T(1,128)}, u32[]{:S(2)}, u32[]{:S(2)}) collective-permute-start(f32[3,10,1,768]{3,2,1,0:T(1,128)} %get-tuple-element.10), channel_id=1, source_target_pairs={{1,0},{2,1},{3,2},{4,3},{5,4},{6,5},{7,6},{8,7},{9,8},{10,9},{11,1... | collective-permute-start | bytes 276488 | tf_op jit(solution)/shard_map/ppermute | solution.py:18
  63.2 4.8 %collective-permute-start.3 = (f32[3,10,1,768]{3,2,1,0:T(1,128)}, f32[3,10,1,768]{3,2,1,0:T(1,128)}, u32[]{:S(2)}, u32[]{:S(2)}) collective-permute-start(f32[3,10,1,768]{3,2,1,0:T(1,128)} %get-tuple-element.11), channel_id=1, source_target_pairs={{0,1},{1,2},{2,3},{3,4},{4,5},{5,6},{6,7},{7,8},{8,9},{9,10},{10,1... | collective-permute-start | bytes 276488 | tf_op jit(solution)/shard_map/ppermute | solution.py:15
  68.1 4.1 %all-to-all-done.1 = bf16[96,3,256]{2,1,0:T(4,128)(2,1)S(1)} async-done(((bf16[96,3,256]{2,1,0:T(4,128)(2,1)}), bf16[96,3,256]{2,1,0:T(4,128)(2,1)S(1)}, u32[]{:S(2)}, u32[]{:S(2)}) %all-to-all-start.1) | async-done | bytes 147488 | tf_op jit(solution)/shard_map/all_to_all | solution.py:40
  72.2 0.8 convert_element_type.25
  73.0 1.4 %broadcast_in_dim.31 = f32[384,3,256]{2,1,0:T(4,128)} broadcast(f32[]{:T(128)} %constant.11.clone.1), dimensions={} | broadcast | bytes 1179652 | tf_op jit(solution)/shard_map/broadcast_in_dim | solution.py:43
  74.4 12.6 %scatter_fusion.1 = f32[384,3,256]{2,1,0:T(4,128)} fusion(f32[384,3,256]{2,1,0:T(4,128)} %broadcast_in_dim.31, s32[96]{0:T(128)S(1)} %reshape.89, f32[96,3,256]{2,1,0:T(4,128)} %convert_element_type.25), kind=kCustom, calls=%fused_computation.4 | custom fusion | flops 73728 | bytes 885120 | tf_op jit(solution)/shard_map/scatter-add | solution.py:43
  87.0 2.6 %copy.18 = f32[3,384,256]{2,1,0:T(8,128)} copy(f32[3,384,256]{2,0,1:T(4,128)} %bitcast.28) | data formatting | bytes 2359296 | tf_op jit(solution)/shard_map/transpose | solution.py:44
  89.6 2.6 %reshape.53 = f32[3,8,16,768]{3,2,1,0:T(8,128)} reshape(f32[3,384,256]{2,1,0:T(8,128)} %copy.18) | data formatting | bytes 2359296 | tf_op jit(solution)/shard_map/reshape | solution.py:44
  92.2 5.3 %multiply_add_fusion = f32[3,8,16,768]{3,2,1,0:T(8,128)} fusion(f32[3,8,16,768]{3,2,1,0:T(8,128)S(1)} %copy-done.1, f32[3,8,16,768]{3,2,1,0:T(8,128)} %reshape.53, f32[3,1,16,768]{3,2,1,0:T(8,128)} %collective-permute-done, f32[3,1,16,768]{3,2,1,0:T(8,128)} %collective-permute-done.1, f32[3,10,16,768]{3,2,1,0:T(8,128)} %copy-done.2, ...), kind=kLoop, calls=%fused_computation.9 | loop fusion | flops 7372800 | bytes 9028608 | tf_op jit(solution)/shard_map/add | solution.py:59
  97.5 1.5 %reshape.54 = bf16[3,384,256]{2,1,0:T(8,128)(2,1)S(1)} reshape(f32[3,8,16,768]{3,2,1,0:T(8,128)} %multiply_add_fusion) | data formatting | bytes 1769472 | tf_op jit(solution)/shard_map/reshape | solution.py:60
  99.0 1.4 %copy.19 = bf16[3,384,256]{2,0,1:T(4,128)(2,1)} copy(bf16[3,384,256]{2,1,0:T(8,128)(2,1)S(1)} %reshape.54) | data formatting | bytes 1179648 | tf_op jit(solution)/shard_map/reshape | solution.py:60
  100.4 1.9 %gather_fusion = bf16[96,3,256]{2,1,0:T(4,128)(2,1)S(1)} fusion(bf16[3,384,256]{2,0,1:T(4,128)(2,1)} %copy.19, s32[1024]{0:T(1024)S(1)} %pad_clamp_fusion.1), kind=kCustom, calls=%fused_computation | custom fusion | bytes 295296 | tf_op jit(solution)/shard_map/jit(_take)/gather | solution.py:61
  102.3 0.8 select_convert_fusion
  103.2 9.8 %all-to-all-start.2 = ((bf16[96,3,256]{2,1,0:T(4,128)(2,1)}), bf16[96,3,256]{2,1,0:T(4,128)(2,1)S(1)}, u32[]{:S(2)}, u32[]{:S(2)}) async-start(bf16[96,3,256]{2,1,0:T(4,128)(2,1)} %select_convert_fusion), calls=%async_computation.2 | async-start | bytes 393216 | tf_op jit(solution)/shard_map/all_to_all | solution.py:62
  113.0 16.6 %all-to-all-done.2 = bf16[96,3,256]{2,1,0:T(4,128)(2,1)S(1)} async-done(((bf16[96,3,256]{2,1,0:T(4,128)(2,1)}), bf16[96,3,256]{2,1,0:T(4,128)(2,1)S(1)}, u32[]{:S(2)}, u32[]{:S(2)}) %all-to-all-start.2) | async-done | bytes 147488 | tf_op jit(solution)/shard_map/all_to_all | solution.py:62
  (28 shorter events, 4.7 us)
Async XLA Ops:
  0.6 35.4 %copy-start = (bf16[32,128,256]{2,1,0:T(8,128)(2,1)S(1)}, bf16[32,128,256]{2,1,0:T(8,128)(2,1)}, u32[]{:S(2)}) copy-start(bf16[32,128,256]{2,1,0:T(8,128)(2,1)} %param.8) | copy-start | bytes 6291460
  4.6 37.9 %all-to-all-start = ((s32[48,2,1]{1,2,0:T(1,128)}), s32[48,2,1]{1,2,0:T(1,128)S(1)}, u32[]{:S(2)}, u32[]{:S(2)}) async-start(s32[48,2,1]{1,2,0:T(1,128)} %bitcast.6), calls=%async_computation | async-start | bytes 49152 | tf_op jit(solution)/shard_map/all_to_all | solution.py:41
  25.8 32.3 %collective-permute-start.1 = (f32[3,1,16,768]{3,2,1,0:T(8,128)}, f32[3,1,16,768]{3,2,1,0:T(8,128)}, u32[]{:S(2)}, u32[]{:S(2)}) collective-permute-start(f32[3,1,16,768]{3,2,1,0:T(8,128)} %get-tuple-element.17), channel_id=1, source_target_pairs={{48,0},{96,48},{144,96},{192,144},{240,192},{288,240},{336,288},{3... | collective-permute-start | bytes 442376 | tf_op jit(solution)/shard_map/ppermute | solution.py:18
  27.1 9.0 %copy-start.3 = (bf16[32,3,128]{2,0,1:T(8,128)(2,1)S(1)}, bf16[32,3,128]{2,0,1:T(8,128)(2,1)}, u32[]{:S(2)}) copy-start(bf16[32,3,128]{2,0,1:T(8,128)(2,1)} %param.7) | copy-start | bytes 73732
  27.1 30.0 %collective-permute-start = (f32[3,1,16,768]{3,2,1,0:T(8,128)}, f32[3,1,16,768]{3,2,1,0:T(8,128)}, u32[]{:S(2)}, u32[]{:S(2)}) collective-permute-start(f32[3,1,16,768]{3,2,1,0:T(8,128)} %get-tuple-element.18), channel_id=1, source_target_pairs={{0,48},{48,96},{96,144},{144,192},{192,240},{240,288},{288,336},{3... | collective-permute-start | bytes 442376 | tf_op jit(solution)/shard_map/ppermute | solution.py:15
  35.3 1.3 copy-start.1
  42.6 29.6 %all-to-all-start.1 = ((bf16[96,3,256]{2,1,0:T(4,128)(2,1)}), bf16[96,3,256]{2,1,0:T(4,128)(2,1)S(1)}, u32[]{:S(2)}, u32[]{:S(2)}) async-start(bf16[96,3,256]{2,1,0:T(4,128)(2,1)} %scatter_fusion), calls=%async_computation.1 | async-start | bytes 393216 | tf_op jit(solution)/shard_map/all_to_all | solution.py:40
  59.0 1.1 copy-start.2
  61.0 31.2 %collective-permute-start.2 = (f32[3,10,1,768]{3,2,1,0:T(1,128)}, f32[3,10,1,768]{3,2,1,0:T(1,128)}, u32[]{:S(2)}, u32[]{:S(2)}) collective-permute-start(f32[3,10,1,768]{3,2,1,0:T(1,128)} %get-tuple-element.10), channel_id=1, source_target_pairs={{1,0},{2,1},{3,2},{4,3},{5,4},{6,5},{7,6},{8,7},{9,8},{10,9},{11,1... | collective-permute-start | bytes 276488 | tf_op jit(solution)/shard_map/ppermute | solution.py:18
  63.2 29.0 %collective-permute-start.3 = (f32[3,10,1,768]{3,2,1,0:T(1,128)}, f32[3,10,1,768]{3,2,1,0:T(1,128)}, u32[]{:S(2)}, u32[]{:S(2)}) collective-permute-start(f32[3,10,1,768]{3,2,1,0:T(1,128)} %get-tuple-element.11), channel_id=1, source_target_pairs={{0,1},{1,2},{2,3},{3,4},{4,5},{5,6},{6,7},{7,8},{8,9},{9,10},{10,1... | collective-permute-start | bytes 276488 | tf_op jit(solution)/shard_map/ppermute | solution.py:15
  103.2 26.4 %all-to-all-start.2 = ((bf16[96,3,256]{2,1,0:T(4,128)(2,1)}), bf16[96,3,256]{2,1,0:T(4,128)(2,1)S(1)}, u32[]{:S(2)}, u32[]{:S(2)}) async-start(bf16[96,3,256]{2,1,0:T(4,128)(2,1)} %select_convert_fusion), calls=%async_computation.2 | async-start | bytes 393216 | tf_op jit(solution)/shard_map/all_to_all | solution.py:62
where the time goes:
time: 132 us; the launch traced here: 131 us
  starting transfers between devices  55.2 us (42%)
  local copies, waits for them, and re-layouts  30.2 us (23%)
  other arithmetic  22.7 us (17%)
  waiting for transfers between devices  20.8 us (16%)
  between operations  1.58 us (1%)
    all_to_all x1, starting transfers between devices, local(): lax.all_to_all(send_ids, 'gy', split_axis=0, concat_axis=0, tiled=True)  19.4 us
    all_to_all x1, waiting for transfers between devices, local(): back = lax.all_to_all(picked, 'gy', split_axis=0, concat_axis=0, tiled=True)  16.6 us
    all_to_all x1, starting transfers between devices, local(): lax.all_to_all(send_blocks, 'gy', split_axis=0, concat_axis=0, tiled=True)  13 us
    scatter-add x1, other arithmetic, local(): jax.ops.segment_sum(got_blocks.astype(jnp.float32), got_ids, num_segments...  12.6 us
    all_to_all x1, starting transfers between devices, local(): back = lax.all_to_all(picked, 'gy', split_axis=0, concat_axis=0, tiled=True)  9.78 us
    ppermute x2, starting transfers between devices, padded_2(): lax.ppermute(lax.slice_in_dim(block, block.shape[dim] - width, None, axis...  9.47 us
    add x1, other arithmetic, local(): fresh = velocity + time_step * (viscosity * lap - adv + force_grid)  5.31 us
    scatter x1, local copies, waits for them, and re-layouts, local(): jnp.zeros((width_gy * room, 3, cells), jnp.bfloat16).at[slot]  4.19 us
  transfers between devices with their start and end apart: 7, of which 2 were waited for; matrix products, arithmetic and copies ran while one was open for 27% of the time, Pallas kernels for 0%

commit v1 on v0

v1 whole, which is shorter than its diff:
```python
import jax
import jax.numpy as jnp
from jax import lax
from jax.experimental import pallas as pl
from jax.experimental.pallas import tpu as pltpu
from jax.sharding import PartitionSpec as P

time_step = 0.25
viscosity = 0.5
F32 = jnp.float32
BF16 = jnp.bfloat16
LANES = 128
ROWS = 8
VMEM = pltpu.VMEM
TRANSPOSED = (((0,), (0,)), ((), ()))
NT = (((1,), (1,)), ((), ()))


def iota(shape, axis):
    return lax.broadcasted_iota(jnp.int32, shape, axis)


def column(row):
    n = row.shape[1]
    same = iota((n, n), 0) == iota((n, n), 1)
    return jnp.sum(jnp.where(same, row, 0), axis=1, keepdims=True)


def dot(a, b, dims=(((1,), (0,)), ((), ()))):
    return lax.dot_general(a, b, dims, preferred_element_type=F32)


def spread(xblocks, counts, forces, kernels, owners, blocks, send, select, product):
    slots = kernels.shape[0]
    comps = forces.shape[0]
    cells = kernels.shape[2]
    room = send.shape[0]
    wide = select.shape[1]
    tall = slots * ROWS
    owner_row = owners[...]
    owner = column(owner_row)
    block = column(blocks[...])
    here = iota((slots, slots), 0)
    there = iota((slots, slots), 1)
    earlier = (owner == owner_row) & (there < here)
    rank = jnp.sum(earlier.astype(jnp.int32), axis=1, keepdims=True)
    live = iota((slots, 1), 0) < counts[0]
    slot = jnp.where(live, owner * 2 + rank, -1)
    choose = (slot == iota((slots, wide), 1)).astype(F32).astype(BF16)
    grow = (iota((tall, slots), 0) // ROWS == iota((tall, slots), 1)).astype(F32).astype(BF16)
    tall_choose = dot(grow, choose)
    select[...] = tall_choose.astype(BF16)
    grow_t = (iota((slots, tall), 1) // ROWS == iota((slots, tall), 0)).astype(F32).astype(BF16)
    wide_choose = dot(choose, grow_t, TRANSPOSED)
    flat = forces[...].reshape(comps * slots, forces.shape[2])
    r = iota((tall, comps * slots), 0)
    s = iota((tall, comps * slots), 1)
    order = ((r % ROWS) * slots + r // ROWS == s).astype(F32).astype(BF16)
    ordered = dot(order, flat)
    for p in range(slots):
        one = ordered[p * ROWS:(p + 1) * ROWS].astype(BF16)
        product[p * ROWS:(p + 1) * ROWS, :] = dot(one, kernels[p])
    made = product[...].astype(BF16)
    lane = iota(wide_choose.shape, 1) % ROWS
    for c in range(comps):
        pick = jnp.where(lane == c, wide_choose, 0.0).astype(BF16)
        send[:, c * cells:(c + 1) * cells] = dot(pick, made)[:room].astype(BF16)
    where = iota((slots, LANES), 1)
    words = jnp.where(where == 0, block // xblocks, jnp.where(where == 1, block % xblocks, jnp.where(where == 2, 1, 0)))
    tags = dot(choose, words.astype(F32).astype(BF16), TRANSPOSED)
    send[:, comps * cells:] = tags[:room].astype(BF16)


def faces(planes, velocity, z_low, z_high, y_low, y_high):
    comps, height, _ = velocity.shape
    rows = height // planes
    for c in range(comps):
        z_low[c] = velocity[c, :rows, :].astype(BF16)
        z_high[c] = velocity[c, height - rows:, :].astype(BF16)
        for out, row in ((y_low, 0), (y_high, rows - 1)):
            picked = [velocity[c, k * rows + row:k * rows + row + 1, :] for k in range(planes)]
            out[c] = jnp.concatenate(picked, axis=0).astype(BF16)


def stencil(planes, velocity, below, above, left, right, base):
    comps, height, xcells = velocity.shape
    rows = height // planes
    x = iota((rows, xcells), 1)
    y = iota((rows, xcells), 0)
    for k in range(planes):
        span = slice(k * rows, (k + 1) * rows)
        center = [velocity[c, span, :] for c in range(comps)]
        for c in range(comps):
            v = center[c]
            x_up = jnp.where(x == xcells - 1, 0.0, pltpu.roll(v, xcells - 1, 1))
            x_down = jnp.where(x == 0, 0.0, pltpu.roll(v, 1, 1))
            y_up = jnp.where(y == rows - 1, right[c, k:k + 1, :].astype(F32), pltpu.roll(v, rows - 1, 0))
            y_down = jnp.where(y == 0, left[c, k:k + 1, :].astype(F32), pltpu.roll(v, 1, 0))
            z_up = velocity[c, (k + 1) * rows:(k + 2) * rows, :] if k + 1 < planes else above[c].astype(F32)
            z_down = velocity[c, (k - 1) * rows:k * rows, :] if k > 0 else below[c].astype(F32)
            lap = x_up + x_down + y_up + y_down + z_up + z_down - 6.0 * v
            adv = (center[0] * (x_up - x_down) + center[1] * (y_up - y_down) + center[2] * (z_up - z_down)) * 0.5
            base[c, span, :] = v + time_step * (viscosity * lap - adv)


def exchange(cells, got, base, fresh, send):
    comps, height, xcells = base.shape
    room = got.shape[0]
    xblocks = xcells // cells
    tags = got[:, comps * cells:].astype(F32)
    row, xb, valid = tags[:, 0:1], tags[:, 1:2], tags[:, 2:3]
    at = iota((room, height), 1).astype(F32)
    match = (row == at) & (valid == 1.0)
    picks = [jnp.where(match & (xb == float(b)), 1.0, 0.0) for b in range(xblocks)]
    narrow = [p.astype(BF16) for p in picks]
    turned = [p.T.astype(BF16) for p in picks]
    for c in range(comps):
        block = got[:, c * cells:(c + 1) * cells]
        total = None
        for b in range(xblocks):
            lanes = slice(b * cells, (b + 1) * cells)
            new = base[c, :, lanes] + time_step * dot(turned[b], block)
            fresh[c, :, lanes] = new
            part = dot(narrow[b], new.astype(BF16))
            total = part if total is None else total + part
        send[:, c * cells:(c + 1) * cells] = total.astype(BF16)


def sample(back, select, kernels, out, result):
    slots = kernels.shape[0]
    cells = kernels.shape[2]
    comps = out.shape[0]
    room = back.shape[0]
    chosen = select[:, :room].astype(F32)
    row = iota(chosen.shape, 0) % ROWS
    total = None
    for c in range(comps):
        pick = jnp.where(row == c, chosen, 0.0).astype(BF16)
        part = dot(pick, back[:, c * cells:(c + 1) * cells])
        total = part if total is None else total + part
    for p in range(slots):
        one = total[p * ROWS:(p + 1) * ROWS].astype(BF16)
        result[p * ROWS:(p + 1) * ROWS, :] = dot(one, kernels[p], NT)
    for c in range(comps):
        out[c] = result[pl.ds(c, slots, stride=ROWS), :]


def call(body, outs, scratch, ins):
    return pl.pallas_call(
        body,
        out_shape=outs,
        in_specs=ins,
        out_specs=[pl.BlockSpec(memory_space=VMEM)] * len(outs),
        scratch_shapes=scratch,
    )


def local(velocity, forces, kernels, owners, blocks, counts):
    width_gy = lax.axis_size("gy")
    width_gz = lax.axis_size("gz")
    slots, comps, points = forces.shape
    cells = kernels.shape[2]
    planes, rows, xcells = velocity.shape[1:]
    xblocks = xcells // cells
    room = width_gy * 2
    wide = -(-room // LANES) * LANES
    payload = comps * cells
    S = jax.ShapeDtypeStruct
    vmem = pl.BlockSpec(memory_space=VMEM)
    smem = pl.BlockSpec(memory_space=pltpu.SMEM)
    grid = velocity.reshape(comps, planes * rows, xcells)

    send, select = call(
        lambda *refs: spread(xblocks, *refs),
        [S((room, payload + LANES), BF16), S((slots * ROWS, wide), BF16)],
        [pltpu.VMEM((slots * ROWS, cells), F32)],
        [smem, vmem, vmem, vmem, vmem],
    )(counts, forces.transpose(1, 0, 2), kernels, owners.reshape(1, slots), blocks.reshape(1, slots))
    got = lax.all_to_all(send.reshape(width_gy, 2, payload + LANES), "gy", split_axis=0, concat_axis=0, tiled=True)
    got = got.reshape(room, payload + LANES)

    z_low, z_high, y_low, y_high = call(
        lambda *refs: faces(planes, *refs),
        [S((comps, rows, xcells), BF16)] * 2 + [S((comps, planes, xcells), BF16)] * 2,
        [],
        [vmem],
    )(grid)
    up_gz = [(i, i + 1) for i in range(width_gz - 1)]
    up_gy = [(i, i + 1) for i in range(width_gy - 1)]
    below = lax.ppermute(z_high, "gz", up_gz)
    above = lax.ppermute(z_low, "gz", [(b, a) for a, b in up_gz])
    left = lax.ppermute(y_high, "gy", up_gy)
    right = lax.ppermute(y_low, "gy", [(b, a) for a, b in up_gy])
    (base,) = call(
        lambda *refs: stencil(planes, *refs),
        [S(grid.shape, F32)],
        [],
        [vmem] * 5,
    )(grid, below, above, left, right)

    fresh, picked = call(
        lambda *refs: exchange(cells, *refs),
        [S(grid.shape, F32), S((room, payload), BF16)],
        [],
        [vmem] * 2,
    )(got, base)
    back = lax.all_to_all(picked.reshape(width_gy, 2, payload), "gy", split_axis=0, concat_axis=0, tiled=True)

    (out,) = call(
        sample,
        [S((comps, slots, points), F32)],
        [pltpu.VMEM((slots * ROWS, points), F32)],
        [vmem] * 3,
    )(back.reshape(room, payload), select, kernels)
    return fresh.reshape(velocity.shape), out.transpose(1, 0, 2)


def solution(mesh):
    return jax.shard_map(
        local,
        mesh=mesh,
        in_specs=(
            P(None, "gz", "gy", None),
            P(("gz", "gy"), None, None),
            P(("gz", "gy"), None, None),
            P(("gz", "gy"), None),
            P(("gz", "gy")),
            P(("gz", "gy")),
        ),
        out_specs=(P(None, "gz", "gy", None), P(("gz", "gy"), None, None)),
        check_vma=False,
    )
```

time: 132 us -> 87.3 us (0.66)
  the two profiles are of different devices: /device:TPU:1 before, /device:TPU:33 now
where the time goes in v1:
time: 87.3 us; the launch traced here: 86.8 us
  starting transfers between devices  33.5 us (38%)
  blocking collectives  26.4 us (30%)
  Pallas kernels  15.2 us (17%)
  local copies, waits for them, and re-layouts  5.35 us (6%)
  waiting for transfers between devices  5.05 us (6%)
  between operations  1.36 us (2%)
    all_to_all x1, blocking collectives, local(): lax.all_to_all(picked.reshape(width_gy, 2, payload), 'gy', split_axis=0,...  26.4 us
    all_to_all x1, starting transfers between devices, local(): lax.all_to_all(send.reshape(width_gy, 2, payload + LANES), 'gy', split_ax...  18.6 us
    ppermute x1, starting transfers between devices, local(): left = lax.ppermute(y_high, 'gy', up_gy)  5.6 us
    ppermute x1, starting transfers between devices, local(): above = lax.ppermute(z_low, 'gz', [(b, a) for a, b in up_gz])  5.17 us
    ppermute x1, waiting for transfers between devices, local(): right = lax.ppermute(y_low, 'gy', [(b, a) for a, b in up_gy])  5.04 us
    pallas_call x1, Pallas kernels, local(): call(lambda *refs: stencil(planes, *refs), [S(grid.shape, F32)], [], [vme...  3.56 us
    pallas_call x1, Pallas kernels, local(): call(sample, [S((comps, slots, points), F32)], [pltpu.VMEM((slots * ROWS,...  3.34 us
    pallas_call x1, Pallas kernels, local(): call(lambda *refs: spread(xblocks, *refs), [S((room, payload + LANES), BF...  3.18 us
  transfers between devices with their start and end apart: 5, of which 1 were waited for; matrix products, arithmetic and copies ran while one was open for 0% of the time, Pallas kernels for 6%

profile of v1, /device:TPU:33, one launch (start us, length us, event | category | flops | bytes accessed | tf_op | source)
XLA Modules:
  0.0 86.8 jit_solution(18413560911702201990)
XLA Ops:
  1.3 3.2 %shard_map.77 = (bf16[96,896]{1,0:T(8,128)(2,1)}, bf16[256,128]{1,0:T(8,128)(2,1)}) custom-call(s32[1]{0:T(128)S(6)} %copy.8.refs_0_, bf16[3,32,128]{2,1,0:T(8,128)(2,1)} %bitcast.9, bf16[32,128,256]{2,1,0:T(8,128)(2,1)} %kernels.1, s32[1,32]{1,0:T(1,128)} %bitcast.10, s32[1,32]{1,0:T(1,128)} %bitcast.11), custom_call_target="tpu_custom_call" | custom-call | tf_op jit(solution)/shard_map/pallas_call | solution.py:173
  4.5 1.7 %reshape.30 = bf16[48,2,896]{2,1,0:T(2,128)(2,1)} reshape(bf16[96,896]{1,0:T(8,128)(2,1)} %get-tuple-element.10) | data formatting | bytes 344064 | tf_op jit(solution)/shard_map/reshape | solution.py:179
  6.1 18.6 %all-to-all-start = ((bf16[48,2,896]{2,1,0:T(2,128)(2,1)}), bf16[48,2,896]{2,1,0:T(2,128)(2,1)S(1)}, u32[]{:S(2)}, u32[]{:S(2)}) async-start(bf16[48,2,896]{2,1,0:T(2,128)(2,1)} %reshape.30), calls=%async_computation | async-start | bytes 344064 | tf_op jit(solution)/shard_map/all_to_all | solution.py:179
  24.7 2.0 %shard_map.78 = (bf16[3,16,768]{2,1,0:T(8,128)(2,1)}, bf16[3,16,768]{2,1,0:T(8,128)(2,1)}, bf16[3,8,768]{2,1,0:T(8,128)(2,1)}, bf16[3,8,768]{2,1,0:T(8,128)(2,1)}) custom-call(f32[3,128,768]{2,1,0:T(8,128)} %bitcast.6), custom_call_target="tpu_custom_call" | custom-call | tf_op jit(solution)/shard_map/pallas_call | solution.py:182
  26.7 2.2 %collective-permute-start = (bf16[3,16,768]{2,1,0:T(8,128)(2,1)}, bf16[3,16,768]{2,1,0:T(8,128)(2,1)S(1)}, u32[]{:S(2)}, u32[]{:S(2)}) collective-permute-start(bf16[3,16,768]{2,1,0:T(8,128)(2,1)} %get-tuple-element.11), channel_id=1, source_target_pairs={{0,48},{48,96},{96,144},{144,192},{192,240},{240,288},{288,336},{3... | collective-permute-start | bytes 221192 | tf_op jit(solution)/shard_map/ppermute | solution.py:190
  29.0 5.2 %collective-permute-start.1 = (bf16[3,16,768]{2,1,0:T(8,128)(2,1)}, bf16[3,16,768]{2,1,0:T(8,128)(2,1)S(1)}, u32[]{:S(2)}, u32[]{:S(2)}) collective-permute-start(bf16[3,16,768]{2,1,0:T(8,128)(2,1)} %get-tuple-element.12), channel_id=1, source_target_pairs={{48,0},{96,48},{144,96},{192,144},{240,192},{288,240},{336,288},{3... | collective-permute-start | bytes 221192 | tf_op jit(solution)/shard_map/ppermute | solution.py:191
  34.1 5.6 %collective-permute-start.2 = (bf16[3,8,768]{2,1,0:T(8,128)(2,1)}, bf16[3,8,768]{2,1,0:T(8,128)(2,1)S(1)}, u32[]{:S(2)}, u32[]{:S(2)}) collective-permute-start(bf16[3,8,768]{2,1,0:T(8,128)(2,1)} %get-tuple-element.13), channel_id=1, source_target_pairs={{0,1},{1,2},{2,3},{3,4},{4,5},{5,6},{6,7},{7,8},{8,9},{9,10},{10,1... | collective-permute-start | bytes 110600 | tf_op jit(solution)/shard_map/ppermute | solution.py:192
  39.8 1.9 %collective-permute-start.3 = (bf16[3,8,768]{2,1,0:T(8,128)(2,1)}, bf16[3,8,768]{2,1,0:T(8,128)(2,1)S(1)}, u32[]{:S(2)}, u32[]{:S(2)}) collective-permute-start(bf16[3,8,768]{2,1,0:T(8,128)(2,1)} %get-tuple-element.14), channel_id=1, source_target_pairs={{1,0},{2,1},{3,2},{4,3},{5,4},{6,5},{7,6},{8,7},{9,8},{10,9},{11,1... | collective-permute-start | bytes 110600 | tf_op jit(solution)/shard_map/ppermute | solution.py:193
  41.7 0.0 collective-permute-done.2.refs_3_
  41.7 0.0 copy-start.2
  41.7 5.0 %collective-permute-done.3.refs_4_ = bf16[3,8,768]{2,1,0:T(8,128)(2,1)S(1)} collective-permute-done((bf16[3,8,768]{2,1,0:T(8,128)(2,1)}, bf16[3,8,768]{2,1,0:T(8,128)(2,1)S(1)}, u32[]{:S(2)}, u32[]{:S(2)}) %collective-permute-start.3) | collective-permute-done | bytes 36896 | tf_op jit(solution)/shard_map/ppermute | solution.py:193
  46.7 0.0 copy-start.3
  46.7 0.0 collective-permute-done.refs_1_
  46.7 0.0 copy-start
  46.8 0.0 collective-permute-done.1.refs_2_
  46.8 0.0 copy-done.2
  46.8 0.6 copy-done.3
  47.4 0.0 copy-done
  47.4 0.0 copy-start.1
  47.4 0.6 copy-done.1
  48.0 3.6 %shard_map.79.refs_1_ = f32[3,128,768]{2,1,0:T(8,128)} custom-call(f32[3,128,768]{2,1,0:T(8,128)} %bitcast.7, bf16[3,16,768]{2,1,0:T(8,128)(2,1)} %copy-done, bf16[3,16,768]{2,1,0:T(8,128)(2,1)} %copy-done.1, bf16[3,8,768]{2,1,0:T(8,128)(2,1)} %copy-done.2, bf16[3,8,768]{2,1,0:T(8,128)(2,1)} %copy-done.3), custom_call_target="tpu_custom_call" | custom-call | tf_op jit(solution)/shard_map/pallas_call | solution.py:194
  51.6 0.0 all-to-all-done
  51.6 0.8 reshape.31.refs_0_
  52.3 3.1 %shard_map.80 = (f32[3,128,768]{2,1,0:T(8,128)}, bf16[96,768]{1,0:T(8,128)(2,1)}) custom-call(bf16[96,896]{1,0:T(8,128)(2,1)} %reshape.31.refs_0_, f32[3,128,768]{2,1,0:T(8,128)} %shard_map.79.refs_1_), custom_call_target="tpu_custom_call" | custom-call | tf_op jit(solution)/shard_map/pallas_call | solution.py:201
  55.4 1.0 %reshape.34 = bf16[48,2,768]{2,1,0:T(2,128)(2,1)S(1)} reshape(bf16[96,768]{1,0:T(8,128)(2,1)} %get-tuple-element.16) | data formatting | bytes 294912 | tf_op jit(solution)/shard_map/reshape | solution.py:207
  56.4 26.4 %all_to_all.10 = bf16[48,2,768]{2,1,0:T(2,128)(2,1)S(1)} all-to-all(bf16[48,2,768]{2,1,0:T(2,128)(2,1)S(1)} %reshape.34), channel_id=1, replica_groups=mesh['gz'=16,'gy'=48] {'gy'}, dimensions={0} | all-to-all | bytes 294912 | tf_op jit(solution)/shard_map/all_to_all | solution.py:207
  82.8 0.7 reshape.35.back
  83.5 3.3 %shard_map.81 = f32[3,32,128]{2,1,0:T(8,128)} custom-call(bf16[96,768]{1,0:T(8,128)(2,1)} %reshape.35.back, bf16[256,128]{1,0:T(8,128)(2,1)} %get-tuple-element.17.select, bf16[32,128,256]{2,1,0:T(8,128)(2,1)} %kernels.1), custom_call_target="tpu_custom_call" | custom-call | tf_op jit(solution)/shard_map/pallas_call | solution.py:209
Async XLA Ops:
  6.1 45.5 %all-to-all-start = ((bf16[48,2,896]{2,1,0:T(2,128)(2,1)}), bf16[48,2,896]{2,1,0:T(2,128)(2,1)S(1)}, u32[]{:S(2)}, u32[]{:S(2)}) async-start(bf16[48,2,896]{2,1,0:T(2,128)(2,1)} %reshape.30), calls=%async_computation | async-start | bytes 344064 | tf_op jit(solution)/shard_map/all_to_all | solution.py:179
  26.7 20.0 %collective-permute-start = (bf16[3,16,768]{2,1,0:T(8,128)(2,1)}, bf16[3,16,768]{2,1,0:T(8,128)(2,1)S(1)}, u32[]{:S(2)}, u32[]{:S(2)}) collective-permute-start(bf16[3,16,768]{2,1,0:T(8,128)(2,1)} %get-tuple-element.11), channel_id=1, source_target_pairs={{0,48},{48,96},{96,144},{144,192},{192,240},{240,288},{288,336},{3... | collective-permute-start | bytes 221192 | tf_op jit(solution)/shard_map/ppermute | solution.py:190
  29.0 17.8 %collective-permute-start.1 = (bf16[3,16,768]{2,1,0:T(8,128)(2,1)}, bf16[3,16,768]{2,1,0:T(8,128)(2,1)S(1)}, u32[]{:S(2)}, u32[]{:S(2)}) collective-permute-start(bf16[3,16,768]{2,1,0:T(8,128)(2,1)} %get-tuple-element.12), channel_id=1, source_target_pairs={{48,0},{96,48},{144,96},{192,144},{240,192},{288,240},{336,288},{3... | collective-permute-start | bytes 221192 | tf_op jit(solution)/shard_map/ppermute | solution.py:191
  34.1 7.5 %collective-permute-start.2 = (bf16[3,8,768]{2,1,0:T(8,128)(2,1)}, bf16[3,8,768]{2,1,0:T(8,128)(2,1)S(1)}, u32[]{:S(2)}, u32[]{:S(2)}) collective-permute-start(bf16[3,8,768]{2,1,0:T(8,128)(2,1)} %get-tuple-element.13), channel_id=1, source_target_pairs={{0,1},{1,2},{2,3},{3,4},{4,5},{5,6},{6,7},{7,8},{8,9},{9,10},{10,1... | collective-permute-start | bytes 110600 | tf_op jit(solution)/shard_map/ppermute | solution.py:192
  39.8 7.0 %collective-permute-start.3 = (bf16[3,8,768]{2,1,0:T(8,128)(2,1)}, bf16[3,8,768]{2,1,0:T(8,128)(2,1)S(1)}, u32[]{:S(2)}, u32[]{:S(2)}) collective-permute-start(bf16[3,8,768]{2,1,0:T(8,128)(2,1)} %get-tuple-element.14), channel_id=1, source_target_pairs={{1,0},{2,1},{3,2},{4,3},{5,4},{6,5},{7,6},{8,7},{9,8},{10,9},{11,1... | collective-permute-start | bytes 110600 | tf_op jit(solution)/shard_map/ppermute | solution.py:193
  41.7 5.1 %copy-start.2 = (bf16[3,8,768]{2,1,0:T(8,128)(2,1)}, bf16[3,8,768]{2,1,0:T(8,128)(2,1)S(1)}, u32[]{:S(2)}) copy-start(bf16[3,8,768]{2,1,0:T(8,128)(2,1)S(1)} %collective-permute-done.2.refs_3_) | copy-start | bytes 110596
  46.7 0.6 copy-start.3
  46.7 0.6 copy-start
  47.4 0.6 copy-start.1

commit v2 on v1

--- a/solution.py
+++ b/solution.py
@@ -4,6 +4,7 @@
 from jax.experimental import pallas as pl
 from jax.experimental.pallas import tpu as pltpu
 from jax.sharding import PartitionSpec as P
+
 
 time_step = 0.25
 viscosity = 0.5
@@ -30,13 +31,29 @@
     return lax.dot_general(a, b, dims, preferred_element_type=F32)
 
 
-def spread(xblocks, counts, forces, kernels, owners, blocks, send, select, product):
+def spread(xblocks, counts, *refs):
+    sources, (send, select, product, kernels), small, arrived = refs[:4], refs[4:8], refs[8:11], refs[11]
+    forces, owners, blocks = small
     slots = kernels.shape[0]
+    parts = arrived.shape[0] - len(small)
+    tables = []
+    for i, (source, target) in enumerate(zip(sources[1:], small)):
+        tables.append(pltpu.make_async_copy(source, target, arrived.at[parts + i]))
+        tables[-1].start()
+    source = sources[0]
+    each = slots // parts
+    copies = []
+    for i in range(parts):
+        span = pl.ds(i * each, each)
+        copies.append(pltpu.make_async_copy(source.at[span], kernels.at[span], arrived.at[i]))
+        copies[-1].start()
     comps = forces.shape[0]
     cells = kernels.shape[2]
     room = send.shape[0]
     wide = select.shape[1]
     tall = slots * ROWS
+    for copy in tables:
+        copy.wait()
     owner_row = owners[...]
     owner = column(owner_row)
     block = column(blocks[...])
@@ -58,6 +75,8 @@
     order = ((r % ROWS) * slots + r // ROWS == s).astype(F32).astype(BF16)
     ordered = dot(order, flat)
     for p in range(slots):
+        if p % each == 0:
+            copies[p // each].wait()
         one = ordered[p * ROWS:(p + 1) * ROWS].astype(BF16)
         product[p * ROWS:(p + 1) * ROWS, :] = dot(one, kernels[p])
     made = product[...].astype(BF16)
@@ -71,20 +90,29 @@
     send[:, comps * cells:] = tags[:room].astype(BF16)
 
 
-def faces(planes, velocity, z_low, z_high, y_low, y_high):
+def even(axis):
+    return lax.axis_index(axis) % 2 == 0
+
+
+def faces(planes, velocity, z_near, z_far, y_near, y_far):
     comps, height, _ = velocity.shape
     rows = height // planes
-    for c in range(comps):
-        z_low[c] = velocity[c, :rows, :].astype(BF16)
-        z_high[c] = velocity[c, height - rows:, :].astype(BF16)
-        for out, row in ((y_low, 0), (y_high, rows - 1)):
-            picked = [velocity[c, k * rows + row:k * rows + row + 1, :] for k in range(planes)]
-            out[c] = jnp.concatenate(picked, axis=0).astype(BF16)
-
-
-def stencil(planes, velocity, below, above, left, right, base):
+    z_even, y_even = even("gz"), even("gy")
+    for c in range(comps):
+        low, high = velocity[c, :rows, :].astype(BF16), velocity[c, height - rows:, :].astype(BF16)
+        z_near[c] = jnp.where(z_even, high, low)
+        z_far[c] = jnp.where(z_even, low, high)
+        low, high = [jnp.concatenate([velocity[c, k * rows + row:k * rows + row + 1, :] for k in range(planes)], axis=0).astype(BF16) for row in (0, rows - 1)]
+        y_near[c] = jnp.where(y_even, high, low)
+        y_far[c] = jnp.where(y_even, low, high)
+
+
+def stencil(planes, velocity, near_side, far_side, base):
     comps, height, xcells = velocity.shape
     rows = height // planes
+    y_even = even("gy")
+    left = [jnp.where(y_even, far_side[c].astype(F32), near_side[c].astype(F32)) for c in range(comps)]
+    right = [jnp.where(y_even, near_side[c].astype(F32), far_side[c].astype(F32)) for c in range(comps)]
     x = iota((rows, xcells), 1)
     y = iota((rows, xcells), 0)
     for k in range(planes):
@@ -94,17 +122,20 @@
             v = center[c]
             x_up = jnp.where(x == xcells - 1, 0.0, pltpu.roll(v, xcells - 1, 1))
             x_down = jnp.where(x == 0, 0.0, pltpu.roll(v, 1, 1))
-            y_up = jnp.where(y == rows - 1, right[c, k:k + 1, :].astype(F32), pltpu.roll(v, rows - 1, 0))
-            y_down = jnp.where(y == 0, left[c, k:k + 1, :].astype(F32), pltpu.roll(v, 1, 0))
-            z_up = velocity[c, (k + 1) * rows:(k + 2) * rows, :] if k + 1 < planes else above[c].astype(F32)
-            z_down = velocity[c, (k - 1) * rows:k * rows, :] if k > 0 else below[c].astype(F32)
+            y_up = jnp.where(y == rows - 1, right[c][k:k + 1, :], pltpu.roll(v, rows - 1, 0))
+            y_down = jnp.where(y == 0, left[c][k:k + 1, :], pltpu.roll(v, 1, 0))
+            z_up = velocity[c, (k + 1) * rows:(k + 2) * rows, :] if k + 1 < planes else 0.0
+            z_down = velocity[c, (k - 1) * rows:k * rows, :] if k > 0 else 0.0
             lap = x_up + x_down + y_up + y_down + z_up + z_down - 6.0 * v
             adv = (center[0] * (x_up - x_down) + center[1] * (y_up - y_down) + center[2] * (z_up - z_down)) * 0.5
             base[c, span, :] = v + time_step * (viscosity * lap - adv)
 
 
-def exchange(cells, got, base, fresh, send):
+def exchange(cells, rows, got, base, velocity, near_side, far_side, fresh, send):
     comps, height, xcells = base.shape
+    z_even = even("gz")
+    below = [jnp.where(z_even, far_side[c].astype(F32), near_side[c].astype(F32)) for c in range(comps)]
+    above = [jnp.where(z_even, near_side[c].astype(F32), far_side[c].astype(F32)) for c in range(comps)]
     room = got.shape[0]
     xblocks = xcells // cells
     tags = got[:, comps * cells:].astype(F32)
@@ -119,7 +150,12 @@
         total = None
         for b in range(xblocks):
             lanes = slice(b * cells, (b + 1) * cells)
-            new = base[c, :, lanes] + time_step * dot(turned[b], block)
+            lift = velocity[comps - 1, :rows, lanes] * (0.5 * time_step) + viscosity * time_step
+            sink = viscosity * time_step - velocity[comps - 1, height - rows:, lanes] * (0.5 * time_step)
+            low = below[c][:, lanes] * lift
+            high = above[c][:, lanes] * sink
+            flow = jnp.concatenate([low + base[c, :rows, lanes], base[c, rows:height - rows, lanes], high + base[c, height - rows:, lanes]], axis=0)
+            new = flow + time_step * dot(turned[b], block)
             fresh[c, :, lanes] = new
             part = dot(narrow[b], new.astype(BF16))
             total = part if total is None else total + part
@@ -145,17 +181,28 @@
         out[c] = result[pl.ds(c, slots, stride=ROWS), :]
 
 
-def call(body, outs, scratch, ins):
+def call(body, outs, scratch, ins, aliases={}):
     return pl.pallas_call(
         body,
         out_shape=outs,
         in_specs=ins,
         out_specs=[pl.BlockSpec(memory_space=VMEM)] * len(outs),
         scratch_shapes=scratch,
+        input_output_aliases=aliases,
+        compiler_params=pltpu.CompilerParams(vmem_limit_bytes=16 * 1024 * 1024),
     )
 
 
-def local(velocity, forces, kernels, owners, blocks, counts):
+def pairs(count, first):
+    low = range(first, count - 1, 2)
+    return [(i, i + 1) for i in low] + [(i + 1, i) for i in low]
+
+
+def near(x):
+    return pltpu.with_memory_space_constraint(x, VMEM)
+
+
+def step(velocity, forces, kernels, owners, blocks, counts):
     width_gy = lax.axis_size("gy")
     width_gz = lax.axis_size("gz")
     slots, comps, points = forces.shape
@@ -165,59 +212,60 @@
     room = width_gy * 2
     wide = -(-room // LANES) * LANES
     payload = comps * cells
-    S = jax.ShapeDtypeStruct
+    parts = 4
+    S = VMEM
     vmem = pl.BlockSpec(memory_space=VMEM)
     smem = pl.BlockSpec(memory_space=pltpu.SMEM)
-    grid = velocity.reshape(comps, planes * rows, xcells)
+    far = pl.BlockSpec(memory_space=pltpu.HBM)
+    grid = near(velocity.reshape(comps, planes * rows, xcells))
 
     send, select = call(
         lambda *refs: spread(xblocks, *refs),
         [S((room, payload + LANES), BF16), S((slots * ROWS, wide), BF16)],
-        [pltpu.VMEM((slots * ROWS, cells), F32)],
-        [smem, vmem, vmem, vmem, vmem],
-    )(counts, forces.transpose(1, 0, 2), kernels, owners.reshape(1, slots), blocks.reshape(1, slots))
+        [VMEM((slots * ROWS, cells), F32), VMEM(kernels.shape, BF16), VMEM((comps, slots, points), BF16), VMEM((1, slots), jnp.int32), VMEM((1, slots), jnp.int32), pltpu.SemaphoreType.DMA((parts + 3,))],
+        [smem] + [far] * 4,
+    )(counts, *[pltpu.with_memory_space_constraint(x, pltpu.HBM) for x in (kernels, forces.transpose(1, 0, 2), owners.reshape(1, slots), blocks.reshape(1, slots))])
     got = lax.all_to_all(send.reshape(width_gy, 2, payload + LANES), "gy", split_axis=0, concat_axis=0, tiled=True)
     got = got.reshape(room, payload + LANES)
 
-    z_low, z_high, y_low, y_high = call(
+    z_near, z_far, y_near, y_far = call(
         lambda *refs: faces(planes, *refs),
         [S((comps, rows, xcells), BF16)] * 2 + [S((comps, planes, xcells), BF16)] * 2,
         [],
         [vmem],
     )(grid)
-    up_gz = [(i, i + 1) for i in range(width_gz - 1)]
-    up_gy = [(i, i + 1) for i in range(width_gy - 1)]
-    below = lax.ppermute(z_high, "gz", up_gz)
-    above = lax.ppermute(z_low, "gz", [(b, a) for a, b in up_gz])
-    left = lax.ppermute(y_high, "gy", up_gy)
-    right = lax.ppermute(y_low, "gy", [(b, a) for a, b in up_gy])
+    y_near = lax.ppermute(y_near, "gy", pairs(width_gy, 0))
+    y_far = lax.ppermute(y_far, "gy", pairs(width_gy, 1))
+    z_near = lax.ppermute(z_near, "gz", pairs(width_gz, 0))
+    z_far = lax.ppermute(z_far, "gz", pairs(width_gz, 1))
     (base,) = call(
         lambda *refs: stencil(planes, *refs),
         [S(grid.shape, F32)],
         [],
-        [vmem] * 5,
-    )(grid, below, above, left, right)
+        [vmem] * 3,
+    )(grid, near(y_near), near(y_far))
 
     fresh, picked = call(
-        lambda *refs: exchange(cells, *refs),
+        lambda *refs: exchange(cells, rows, *refs),
         [S(grid.shape, F32), S((room, payload), BF16)],
         [],
-        [vmem] * 2,
-    )(got, base)
+        [vmem] * 5,
+        {1: 0},
+    )(near(got), near(base), grid, near(z_near), near(z_far))
     back = lax.all_to_all(picked.reshape(width_gy, 2, payload), "gy", split_axis=0, concat_axis=0, tiled=True)
 
     (out,) = call(
         sample,
-        [S((comps, slots, points), F32)],
-        [pltpu.VMEM((slots * ROWS, points), F32)],
+        [jax.ShapeDtypeStruct((comps, slots, points), F32)],
+        [VMEM((slots * ROWS, points), F32)],
         [vmem] * 3,
-    )(back.reshape(room, payload), select, kernels)
+    )(near(back.reshape(room, payload)), near(select), near(kernels))
     return fresh.reshape(velocity.shape), out.transpose(1, 0, 2)
 
 
 def solution(mesh):
     return jax.shard_map(
-        local,
+        step,
         mesh=mesh,
         in_specs=(
             P(None, "gz", "gy", None),

time: 87.3 us -> 73.5 us (0.84)
  the two profiles are of different devices: /device:TPU:33 before, /device:TPU:27 now
where the time goes in v2:
time: 73.5 us; the launch traced here: 73.1 us
  starting transfers between devices  46.8 us (64%)
  waiting for transfers between devices  16.1 us (22%)
  Pallas kernels  6.13 us (8%)
  local copies, waits for them, and re-layouts  2.61 us (4%)
  between operations  1.43 us (2%)
    all_to_all x1, starting transfers between devices, step(): lax.all_to_all(send.reshape(width_gy, 2, payload + LANES), 'gy', split_ax...  17.7 us
    all_to_all x1, waiting for transfers between devices, step(): lax.all_to_all(picked.reshape(width_gy, 2, payload), 'gy', split_axis=0,...  14.1 us
    all_to_all x1, starting transfers between devices, step(): lax.all_to_all(picked.reshape(width_gy, 2, payload), 'gy', split_axis=0,...  14 us
    ppermute x1, starting transfers between devices, step(): y_far = lax.ppermute(y_far, 'gy', pairs(width_gy, 1))  4.71 us
    ppermute x1, starting transfers between devices, step(): z_far = lax.ppermute(z_far, 'gz', pairs(width_gz, 1))  4.44 us
    ppermute x1, starting transfers between devices, step(): z_near = lax.ppermute(z_near, 'gz', pairs(width_gz, 0))  3.06 us
    ppermute x1, starting transfers between devices, step(): y_near = lax.ppermute(y_near, 'gy', pairs(width_gy, 0))  2.81 us
    pallas_call x1, Pallas kernels, step(): call(lambda *refs: spread(xblocks, *refs), [S((room, payload + LANES), BF...  2.24 us
  transfers between devices with their start and end apart: 6, of which 2 were waited for; matrix products, arithmetic and copies ran while one was open for 1% of the time, Pallas kernels for 2%

profile of v2, /device:TPU:27, one launch (start us, length us, event | category | flops | bytes accessed | tf_op | source)
XLA Modules:
  0.0 73.1 jit_solution(2197065634363485965)
XLA Ops:
  1.3 0.0 copy-start
  1.3 2.2 %shard_map.77 = (bf16[96,896]{1,0:T(8,128)(2,1)S(1)}, bf16[256,128]{1,0:T(8,128)(2,1)S(1)}) custom-call(s32[1]{0:T(128)S(6)} %copy.11.refs_0_, bf16[32,128,256]{2,1,0:T(8,128)(2,1)} %kernels.1, bf16[3,32,128]{2,1,0:T(8,128)(2,1)} %bitcast.11, s32[1,32]{1,0:T(1,128)} %bitcast.12, s32[1,32]{1,0:T(1,128)} %bitcast.13), custom_call_target="tpu_custom_call" | custom-call | tf_op jit(solution)/shard_map/pallas_call | solution.py:222
  3.5 0.7 %reshape.30 = bf16[48,2,896]{2,1,0:T(2,128)(2,1)} reshape(bf16[96,896]{1,0:T(8,128)(2,1)S(1)} %get-tuple-element.10) | data formatting | bytes 344064 | tf_op jit(solution)/shard_map/reshape | solution.py:228
  4.3 17.7 %all-to-all-start = ((bf16[48,2,896]{2,1,0:T(2,128)(2,1)}), bf16[48,2,896]{2,1,0:T(2,128)(2,1)S(1)}, u32[]{:S(2)}, u32[]{:S(2)}) async-start(bf16[48,2,896]{2,1,0:T(2,128)(2,1)} %reshape.30), calls=%async_computation | async-start | bytes 344064 | tf_op jit(solution)/shard_map/all_to_all | solution.py:228
  22.0 0.0 copy-done
  22.0 0.1 shard_map.78
  22.1 3.1 %collective-permute-start.2 = (bf16[3,16,768]{2,1,0:T(8,128)(2,1)S(1)}, bf16[3,16,768]{2,1,0:T(8,128)(2,1)S(1)}, u32[]{:S(2)}, u32[]{:S(2)}) collective-permute-start(bf16[3,16,768]{2,1,0:T(8,128)(2,1)S(1)} %get-tuple-element.13), channel_id=1, source_target_pairs={{0,48},{96,144},{192,240},{288,336},{384,432},{480,528},{576,624},... | collective-permute-start | bytes 221192 | tf_op jit(solution)/shard_map/ppermute | solution.py:239
  25.2 4.4 %collective-permute-start.3 = (bf16[3,16,768]{2,1,0:T(8,128)(2,1)S(1)}, bf16[3,16,768]{2,1,0:T(8,128)(2,1)S(1)}, u32[]{:S(2)}, u32[]{:S(2)}) collective-permute-start(bf16[3,16,768]{2,1,0:T(8,128)(2,1)S(1)} %get-tuple-element.14), channel_id=1, source_target_pairs={{48,96},{144,192},{240,288},{336,384},{432,480},{528,576},{624,672... | collective-permute-start | bytes 221192 | tf_op jit(solution)/shard_map/ppermute | solution.py:240
  29.7 2.8 %collective-permute-start = (bf16[3,8,768]{2,1,0:T(8,128)(2,1)S(1)}, bf16[3,8,768]{2,1,0:T(8,128)(2,1)S(1)}, u32[]{:S(2)}, u32[]{:S(2)}) collective-permute-start(bf16[3,8,768]{2,1,0:T(8,128)(2,1)S(1)} %get-tuple-element.11), channel_id=1, source_target_pairs={{0,1},{2,3},{4,5},{6,7},{8,9},{10,11},{12,13},{14,15},{16,17},{18,... | collective-permute-start | bytes 110600 | tf_op jit(solution)/shard_map/ppermute | solution.py:237
  32.5 4.7 %collective-permute-start.1 = (bf16[3,8,768]{2,1,0:T(8,128)(2,1)S(1)}, bf16[3,8,768]{2,1,0:T(8,128)(2,1)S(1)}, u32[]{:S(2)}, u32[]{:S(2)}) collective-permute-start(bf16[3,8,768]{2,1,0:T(8,128)(2,1)S(1)} %get-tuple-element.12), channel_id=1, source_target_pairs={{1,2},{3,4},{5,6},{7,8},{9,10},{11,12},{13,14},{15,16},{17,18},{19... | collective-permute-start | bytes 110600 | tf_op jit(solution)/shard_map/ppermute | solution.py:238
  37.2 0.0 collective-permute-done.refs_1_
  37.2 2.1 %collective-permute-done.1.refs_2_ = bf16[3,8,768]{2,1,0:T(8,128)(2,1)S(1)} collective-permute-done((bf16[3,8,768]{2,1,0:T(8,128)(2,1)S(1)}, bf16[3,8,768]{2,1,0:T(8,128)(2,1)S(1)}, u32[]{:S(2)}, u32[]{:S(2)}) %collective-permute-start.1) | collective-permute-done | bytes 36896 | tf_op jit(solution)/shard_map/ppermute | solution.py:238
  39.3 1.1 %shard_map.79.refs_1_ = f32[3,128,768]{2,1,0:T(8,128)S(1)} custom-call(f32[3,128,768]{2,1,0:T(8,128)S(1)} %bitcast.8, bf16[3,8,768]{2,1,0:T(8,128)(2,1)S(1)} %collective-permute-done.refs_1_, bf16[3,8,768]{2,1,0:T(8,128)(2,1)S(1)} %collective-permute-done.1.refs_2_), custom_call_target="tpu_custom_call" | custom-call | tf_op jit(solution)/shard_map/pallas_call | solution.py:241
  40.4 0.0 all-to-all-done
  40.4 0.1 reshape.31.refs_0_
  40.5 0.0 collective-permute-done.2.refs_3_
  40.5 0.0 collective-permute-done.3.refs_4_
  40.5 1.0 %shard_map.80 = (f32[3,128,768]{2,1,0:T(8,128)S(1)}, bf16[96,768]{1,0:T(8,128)(2,1)S(1)}) custom-call(bf16[96,896]{1,0:T(8,128)(2,1)S(1)} %reshape.31.refs_0_, f32[3,128,768]{2,1,0:T(8,128)S(1)} %shard_map.79.refs_1_, f32[3,128,768]{2,1,0:T(8,128)S(1)} %bitcast.9, ...), custom_call_target="tpu_custom_call", output_to_operand_aliasing={{0}: (1, {})} | custom-call | tf_op jit(solution)/shard_map/pallas_call | solution.py:248
  41.5 0.7 reshape.34
  42.3 14.0 %all-to-all-start.1 = ((bf16[48,2,768]{2,1,0:T(2,128)(2,1)}), bf16[48,2,768]{2,1,0:T(2,128)(2,1)S(1)}, u32[]{:S(2)}, u32[]{:S(2)}) async-start(bf16[48,2,768]{2,1,0:T(2,128)(2,1)} %reshape.34), calls=%async_computation.1 | async-start | bytes 294912 | tf_op jit(solution)/shard_map/all_to_all | solution.py:255
  56.3 0.0 copy-start.1
  56.3 1.0 %copy.10 = f32[3,8,16,768]{3,2,1,0:T(8,128)} copy(f32[3,8,16,768]{3,2,1,0:T(8,128)S(1)} %bitcast.6) | data formatting | bytes 2359296
  57.3 14.1 %all-to-all-done.1 = bf16[48,2,768]{2,1,0:T(2,128)(2,1)S(1)} async-done(((bf16[48,2,768]{2,1,0:T(2,128)(2,1)}), bf16[48,2,768]{2,1,0:T(2,128)(2,1)S(1)}, u32[]{:S(2)}, u32[]{:S(2)}) %all-to-all-start.1) | async-done | bytes 147488 | tf_op jit(solution)/shard_map/all_to_all | solution.py:255
  71.4 0.1 reshape.35.back
  71.5 0.0 copy-done.1
  71.5 1.6 %shard_map.81 = f32[3,32,128]{2,1,0:T(8,128)} custom-call(bf16[96,768]{1,0:T(8,128)(2,1)S(1)} %reshape.35.back, bf16[256,128]{1,0:T(8,128)(2,1)S(1)} %get-tuple-element.17.select, bf16[32,128,256]{2,1,0:T(8,128)(2,1)S(1)} %copy-done.1), custom_call_target="tpu_custom_call" | custom-call | tf_op jit(solution)/shard_map/pallas_call | solution.py:257
Async XLA Ops:
  1.3 20.7 %copy-start = (f32[3,8,16,768]{3,2,1,0:T(8,128)S(1)}, f32[3,8,16,768]{3,2,1,0:T(8,128)}, u32[]{:S(2)}) copy-start(f32[3,8,16,768]{3,2,1,0:T(8,128)} %param.6) | copy-start | bytes 3538948
  4.3 36.1 %all-to-all-start = ((bf16[48,2,896]{2,1,0:T(2,128)(2,1)}), bf16[48,2,896]{2,1,0:T(2,128)(2,1)S(1)}, u32[]{:S(2)}, u32[]{:S(2)}) async-start(bf16[48,2,896]{2,1,0:T(2,128)(2,1)} %reshape.30), calls=%async_computation | async-start | bytes 344064 | tf_op jit(solution)/shard_map/all_to_all | solution.py:228
  22.1 18.3 %collective-permute-start.2 = (bf16[3,16,768]{2,1,0:T(8,128)(2,1)S(1)}, bf16[3,16,768]{2,1,0:T(8,128)(2,1)S(1)}, u32[]{:S(2)}, u32[]{:S(2)}) collective-permute-start(bf16[3,16,768]{2,1,0:T(8,128)(2,1)S(1)} %get-tuple-element.13), channel_id=1, source_target_pairs={{0,48},{96,144},{192,240},{288,336},{384,432},{480,528},{576,624},... | collective-permute-start | bytes 221192 | tf_op jit(solution)/shard_map/ppermute | solution.py:239
  25.2 15.3 %collective-permute-start.3 = (bf16[3,16,768]{2,1,0:T(8,128)(2,1)S(1)}, bf16[3,16,768]{2,1,0:T(8,128)(2,1)S(1)}, u32[]{:S(2)}, u32[]{:S(2)}) collective-permute-start(bf16[3,16,768]{2,1,0:T(8,128)(2,1)S(1)} %get-tuple-element.14), channel_id=1, source_target_pairs={{48,96},{144,192},{240,288},{336,384},{432,480},{528,576},{624,672... | collective-permute-start | bytes 221192 | tf_op jit(solution)/shard_map/ppermute | solution.py:240
  29.7 7.5 %collective-permute-start = (bf16[3,8,768]{2,1,0:T(8,128)(2,1)S(1)}, bf16[3,8,768]{2,1,0:T(8,128)(2,1)S(1)}, u32[]{:S(2)}, u32[]{:S(2)}) collective-permute-start(bf16[3,8,768]{2,1,0:T(8,128)(2,1)S(1)} %get-tuple-element.11), channel_id=1, source_target_pairs={{0,1},{2,3},{4,5},{6,7},{8,9},{10,11},{12,13},{14,15},{16,17},{18,... | collective-permute-start | bytes 110600 | tf_op jit(solution)/shard_map/ppermute | solution.py:237
  32.5 6.8 %collective-permute-start.1 = (bf16[3,8,768]{2,1,0:T(8,128)(2,1)S(1)}, bf16[3,8,768]{2,1,0:T(8,128)(2,1)S(1)}, u32[]{:S(2)}, u32[]{:S(2)}) collective-permute-start(bf16[3,8,768]{2,1,0:T(8,128)(2,1)S(1)} %get-tuple-element.12), channel_id=1, source_target_pairs={{1,2},{3,4},{5,6},{7,8},{9,10},{11,12},{13,14},{15,16},{17,18},{19... | collective-permute-start | bytes 110600 | tf_op jit(solution)/shard_map/ppermute | solution.py:238
  42.3 29.2 %all-to-all-start.1 = ((bf16[48,2,768]{2,1,0:T(2,128)(2,1)}), bf16[48,2,768]{2,1,0:T(2,128)(2,1)S(1)}, u32[]{:S(2)}, u32[]{:S(2)}) async-start(bf16[48,2,768]{2,1,0:T(2,128)(2,1)} %reshape.34), calls=%async_computation.1 | async-start | bytes 294912 | tf_op jit(solution)/shard_map/all_to_all | solution.py:255
  56.3 15.2 %copy-start.1 = (bf16[32,128,256]{2,1,0:T(8,128)(2,1)S(1)}, bf16[32,128,256]{2,1,0:T(8,128)(2,1)}, u32[]{:S(2)}) copy-start(bf16[32,128,256]{2,1,0:T(8,128)(2,1)} %kernels.1) | copy-start | bytes 6291460

commit v3 on v2

--- a/solution.py
+++ b/solution.py
@@ -49,7 +49,7 @@
         copies[-1].start()
     comps = forces.shape[0]
     cells = kernels.shape[2]
-    room = send.shape[0]
+    room = send.shape[0] * send.shape[1]
     wide = select.shape[1]
     tall = slots * ROWS
     for copy in tables:
@@ -83,18 +83,18 @@
     lane = iota(wide_choose.shape, 1) % ROWS
     for c in range(comps):
         pick = jnp.where(lane == c, wide_choose, 0.0).astype(BF16)
-        send[:, c * cells:(c + 1) * cells] = dot(pick, made)[:room].astype(BF16)
+        send[:, :, c * cells:(c + 1) * cells] = dot(pick, made)[:room].reshape(room // 2, 2, cells).astype(BF16)
     where = iota((slots, LANES), 1)
     words = jnp.where(where == 0, block // xblocks, jnp.where(where == 1, block % xblocks, jnp.where(where == 2, 1, 0)))
     tags = dot(choose, words.astype(F32).astype(BF16), TRANSPOSED)
-    send[:, comps * cells:] = tags[:room].astype(BF16)
+    send[:, :, comps * cells:] = tags[:room].reshape(room // 2, 2, LANES).astype(BF16)
 
 
 def even(axis):
     return lax.axis_index(axis) % 2 == 0
 
 
-def faces(planes, velocity, z_near, z_far, y_near, y_far):
+def faces(planes, velocity, z_near, z_far, y_near, y_far, lifts):
     comps, height, _ = velocity.shape
     rows = height // planes
     z_even, y_even = even("gz"), even("gy")
@@ -102,17 +102,18 @@
         low, high = velocity[c, :rows, :].astype(BF16), velocity[c, height - rows:, :].astype(BF16)
         z_near[c] = jnp.where(z_even, high, low)
         z_far[c] = jnp.where(z_even, low, high)
-        low, high = [jnp.concatenate([velocity[c, k * rows + row:k * rows + row + 1, :] for k in range(planes)], axis=0).astype(BF16) for row in (0, rows - 1)]
+        first, last = [jnp.concatenate([velocity[c, k * rows + row:k * rows + row + 1, :] for k in range(planes)], axis=0) for row in (0, rows - 1)]
+        if c == 1:
+            lifts[0] = viscosity + 0.5 * first
+            lifts[1] = viscosity - 0.5 * last
+        low, high = first.astype(BF16), last.astype(BF16)
         y_near[c] = jnp.where(y_even, high, low)
         y_far[c] = jnp.where(y_even, low, high)
 
 
-def stencil(planes, velocity, near_side, far_side, base):
+def stencil(planes, velocity, base):
     comps, height, xcells = velocity.shape
     rows = height // planes
-    y_even = even("gy")
-    left = [jnp.where(y_even, far_side[c].astype(F32), near_side[c].astype(F32)) for c in range(comps)]
-    right = [jnp.where(y_even, near_side[c].astype(F32), far_side[c].astype(F32)) for c in range(comps)]
     x = iota((rows, xcells), 1)
     y = iota((rows, xcells), 0)
     for k in range(planes):
@@ -122,8 +123,8 @@
             v = center[c]
             x_up = jnp.where(x == xcells - 1, 0.0, pltpu.roll(v, xcells - 1, 1))
             x_down = jnp.where(x == 0, 0.0, pltpu.roll(v, 1, 1))
-            y_up = jnp.where(y == rows - 1, right[c][k:k + 1, :], pltpu.roll(v, rows - 1, 0))
-            y_down = jnp.where(y == 0, left[c][k:k + 1, :], pltpu.roll(v, 1, 0))
+            y_up = jnp.where(y == rows - 1, 0.0, pltpu.roll(v, rows - 1, 0))
+            y_down = jnp.where(y == 0, 0.0, pltpu.roll(v, 1, 0))
             z_up = velocity[c, (k + 1) * rows:(k + 2) * rows, :] if k + 1 < planes else 0.0
             z_down = velocity[c, (k - 1) * rows:k * rows, :] if k > 0 else 0.0
             lap = x_up + x_down + y_up + y_down + z_up + z_down - 6.0 * v
@@ -131,35 +132,42 @@
             base[c, span, :] = v + time_step * (viscosity * lap - adv)
 
 
-def exchange(cells, rows, got, base, velocity, near_side, far_side, fresh, send):
+def exchange(cells, planes, got, base, velocity, lifts, y_near, y_far, z_near, z_far, fresh, send):
     comps, height, xcells = base.shape
-    z_even = even("gz")
-    below = [jnp.where(z_even, far_side[c].astype(F32), near_side[c].astype(F32)) for c in range(comps)]
-    above = [jnp.where(z_even, near_side[c].astype(F32), far_side[c].astype(F32)) for c in range(comps)]
+    rows = height // planes
     room = got.shape[0]
     xblocks = xcells // cells
+    y_even, z_even = even("gy"), even("gz")
     tags = got[:, comps * cells:].astype(F32)
     row, xb, valid = tags[:, 0:1], tags[:, 1:2], tags[:, 2:3]
     at = iota((room, height), 1).astype(F32)
     match = (row == at) & (valid == 1.0)
     picks = [jnp.where(match & (xb == float(b)), 1.0, 0.0) for b in range(xblocks)]
     narrow = [p.astype(BF16) for p in picks]
-    turned = [p.T.astype(BF16) for p in picks]
-    for c in range(comps):
-        block = got[:, c * cells:(c + 1) * cells]
+    edge = iota((4 * planes, height), 0) % (2 * planes)
+    spot = (edge % planes) * rows + jnp.where(edge >= planes, rows - 1, 0)
+    edges = jnp.where(iota((4 * planes, height), 1) == spot, 1.0, 0.0)
+    turned = [jnp.concatenate([p, edges], axis=0).T.astype(BF16) for p in picks]
+    lift = velocity[comps - 1, :rows, :] * (0.5 * time_step) + viscosity * time_step
+    sink = viscosity * time_step - velocity[comps - 1, height - rows:, :] * (0.5 * time_step)
+    for c in range(comps):
+        one, two = z_near[c].astype(F32), z_far[c].astype(F32)
+        low = jnp.where(z_even, two, one) * lift
+        high = jnp.where(z_even, one, two) * sink
+        one, two = y_near[c].astype(F32), y_far[c].astype(F32)
+        sides = jnp.concatenate([jnp.where(y_even, two, one) * lifts[0], jnp.where(y_even, one, two) * lifts[1]], axis=0)
+        coarse = sides.astype(BF16)
+        fine = (sides - coarse.astype(F32)).astype(BF16)
         total = None
         for b in range(xblocks):
             lanes = slice(b * cells, (b + 1) * cells)
-            lift = velocity[comps - 1, :rows, lanes] * (0.5 * time_step) + viscosity * time_step
-            sink = viscosity * time_step - velocity[comps - 1, height - rows:, lanes] * (0.5 * time_step)
-            low = below[c][:, lanes] * lift
-            high = above[c][:, lanes] * sink
-            flow = jnp.concatenate([low + base[c, :rows, lanes], base[c, rows:height - rows, lanes], high + base[c, height - rows:, lanes]], axis=0)
+            block = jnp.concatenate([got[:, c * cells:(c + 1) * cells], coarse[:, lanes], fine[:, lanes]], axis=0)
+            flow = jnp.concatenate([low[:, lanes] + base[c, :rows, lanes], base[c, rows:height - rows, lanes], high[:, lanes] + base[c, height - rows:, lanes]], axis=0)
             new = flow + time_step * dot(turned[b], block)
             fresh[c, :, lanes] = new
             part = dot(narrow[b], new.astype(BF16))
             total = part if total is None else total + part
-        send[:, c * cells:(c + 1) * cells] = total.astype(BF16)
+        send[:, :, c * cells:(c + 1) * cells] = total.reshape(send.shape[0], 2, cells).astype(BF16)
 
 
 def sample(back, select, kernels, out, result):
@@ -215,22 +223,21 @@
     parts = 4
     S = VMEM
     vmem = pl.BlockSpec(memory_space=VMEM)
-    smem = pl.BlockSpec(memory_space=pltpu.SMEM)
     far = pl.BlockSpec(memory_space=pltpu.HBM)
     grid = near(velocity.reshape(comps, planes * rows, xcells))
 
     send, select = call(
         lambda *refs: spread(xblocks, *refs),
-        [S((room, payload + LANES), BF16), S((slots * ROWS, wide), BF16)],
+        [S((width_gy, 2, payload + LANES), BF16), S((slots * ROWS, wide), BF16)],
         [VMEM((slots * ROWS, cells), F32), VMEM(kernels.shape, BF16), VMEM((comps, slots, points), BF16), VMEM((1, slots), jnp.int32), VMEM((1, slots), jnp.int32), pltpu.SemaphoreType.DMA((parts + 3,))],
-        [smem] + [far] * 4,
+        [pl.BlockSpec(memory_space=pltpu.SMEM)] + [far] * 4,
     )(counts, *[pltpu.with_memory_space_constraint(x, pltpu.HBM) for x in (kernels, forces.transpose(1, 0, 2), owners.reshape(1, slots), blocks.reshape(1, slots))])
-    got = lax.all_to_all(send.reshape(width_gy, 2, payload + LANES), "gy", split_axis=0, concat_axis=0, tiled=True)
+    got = lax.all_to_all(send, "gy", split_axis=0, concat_axis=0, tiled=True)
     got = got.reshape(room, payload + LANES)
 
-    z_near, z_far, y_near, y_far = call(
+    z_near, z_far, y_near, y_far, lifts = call(
         lambda *refs: faces(planes, *refs),
-        [S((comps, rows, xcells), BF16)] * 2 + [S((comps, planes, xcells), BF16)] * 2,
+        [S((comps, rows, xcells), BF16)] * 2 + [S((comps, planes, xcells), BF16)] * 2 + [S((2, planes, xcells), F32)],
         [],
         [vmem],
     )(grid)
@@ -242,17 +249,17 @@
         lambda *refs: stencil(planes, *refs),
         [S(grid.shape, F32)],
         [],
-        [vmem] * 3,
-    )(grid, near(y_near), near(y_far))
+        [vmem],
+    )(grid)
 
     fresh, picked = call(
-        lambda *refs: exchange(cells, rows, *refs),
-        [S(grid.shape, F32), S((room, payload), BF16)],
+        lambda *refs: exchange(cells, planes, *refs),
+        [S(grid.shape, F32), S((width_gy, 2, payload), BF16)],
         [],
-        [vmem] * 5,
+        [vmem] * 8,
         {1: 0},
-    )(near(got), near(base), grid, near(z_near), near(z_far))
-    back = lax.all_to_all(picked.reshape(width_gy, 2, payload), "gy", split_axis=0, concat_axis=0, tiled=True)
+    )(near(got), near(base), grid, near(lifts), near(y_near), near(y_far), near(z_near), near(z_far))
+    back = lax.all_to_all(picked, "gy", split_axis=0, concat_axis=0, tiled=True)
 
     (out,) = call(
         sample,

time: 73.5 us -> 72.2 us (0.982)
  local copies, waits for them, and re-layouts: 2.61 us -> 1.15 us
  Pallas kernels: 6.13 us -> 7.49 us
  waiting for transfers between devices: 16.1 us -> 15 us
    reshape x2 -> x0, local copies, waits for them, and re-layouts: 1.46 us -> none  [the longest x1 0.74 us: step(): send.reshape(width_gy, 2, payload + LANES)]
    pallas_call x3, Pallas kernels: 4.39 us -> 5.74 us  [the longest x1 2.97 us: step(): call(lambda *refs: spread(xblocks, *refs), [S((width_gy, 2, payload + LAN...]
    ppermute x1, waiting for transfers between devices: 2.05 us -> 0.87 us  [step(): y_far = lax.ppermute(y_far, 'gy', pairs(width_gy, 1))]
  transfers between devices with their start and end apart: 6 -> 6, of which waited for: 2 -> 2; matrix products, arithmetic and copies ran while one was open for 1% -> 2% of each run, Pallas kernels for 2% -> 2%
where the time goes in v3:
time: 72.2 us; the launch traced here: 71.8 us
  starting transfers between devices  46.8 us (65%)
  waiting for transfers between devices  15 us (21%)
  Pallas kernels  7.49 us (10%)
  between operations  1.41 us (2%)
  local copies, waits for them, and re-layouts  1.15 us (2%)
    all_to_all x1, starting transfers between devices, step(): got = lax.all_to_all(send, 'gy', split_axis=0, concat_axis=0, tiled=True)  17.7 us
    all_to_all x1, waiting for transfers between devices, step(): back = lax.all_to_all(picked, 'gy', split_axis=0, concat_axis=0, tiled=True)  14.1 us
    all_to_all x1, starting transfers between devices, step(): back = lax.all_to_all(picked, 'gy', split_axis=0, concat_axis=0, tiled=True)  14 us
    ppermute x1, starting transfers between devices, step(): y_far = lax.ppermute(y_far, 'gy', pairs(width_gy, 1))  4.71 us
    ppermute x1, starting transfers between devices, step(): z_far = lax.ppermute(z_far, 'gz', pairs(width_gz, 1))  4.44 us
    ppermute x1, starting transfers between devices, step(): z_near = lax.ppermute(z_near, 'gz', pairs(width_gz, 0))  3.06 us
    pallas_call x1, Pallas kernels, step(): call(lambda *refs: spread(xblocks, *refs), [S((width_gy, 2, payload + LAN...  2.97 us
    ppermute x1, starting transfers between devices, step(): y_near = lax.ppermute(y_near, 'gy', pairs(width_gy, 0))  2.81 us
  transfers between devices with their start and end apart: 6, of which 2 were waited for; matrix products, arithmetic and copies ran while one was open for 2% of the time, Pallas kernels for 2%

profile of v3, /device:TPU:27, one launch (start us, length us, event | category | flops | bytes accessed | tf_op | source)
XLA Modules:
  0.0 71.8 jit_solution(13879530974917188757)
XLA Ops:
  1.3 0.0 copy-start
  1.3 3.0 %shard_map.77 = (bf16[48,2,896]{2,1,0:T(2,128)(2,1)}, bf16[256,128]{1,0:T(8,128)(2,1)S(1)}) custom-call(s32[1]{0:T(128)S(6)} %copy.11.refs_0_, bf16[32,128,256]{2,1,0:T(8,128)(2,1)} %kernels.1, bf16[3,32,128]{2,1,0:T(8,128)(2,1)} %bitcast.11, s32[1,32]{1,0:T(1,128)} %bitcast.12, s32[1,32]{1,0:T(1,128)} %bitcast.13), custom_call_target="tpu_custom_call" | custom-call | tf_op jit(solution)/shard_map/pallas_call | solution.py:229
  4.3 17.7 %all-to-all-start = ((bf16[48,2,896]{2,1,0:T(2,128)(2,1)}), bf16[48,2,896]{2,1,0:T(2,128)(2,1)S(1)}, u32[]{:S(2)}, u32[]{:S(2)}) async-start(bf16[48,2,896]{2,1,0:T(2,128)(2,1)} %get-tuple-element.11), calls=%async_computation | async-start | bytes 344064 | tf_op jit(solution)/shard_map/all_to_all | solution.py:235
  22.0 0.0 copy-done
  22.0 0.1 shard_map.79
  22.1 3.1 %collective-permute-start.2 = (bf16[3,16,768]{2,1,0:T(8,128)(2,1)S(1)}, bf16[3,16,768]{2,1,0:T(8,128)(2,1)S(1)}, u32[]{:S(2)}, u32[]{:S(2)}) collective-permute-start(bf16[3,16,768]{2,1,0:T(8,128)(2,1)S(1)} %get-tuple-element.15), channel_id=1, source_target_pairs={{0,48},{96,144},{192,240},{288,336},{384,432},{480,528},{576,624},... | collective-permute-start | bytes 221192 | tf_op jit(solution)/shard_map/ppermute | solution.py:246
  25.2 4.4 %collective-permute-start.3 = (bf16[3,16,768]{2,1,0:T(8,128)(2,1)S(1)}, bf16[3,16,768]{2,1,0:T(8,128)(2,1)S(1)}, u32[]{:S(2)}, u32[]{:S(2)}) collective-permute-start(bf16[3,16,768]{2,1,0:T(8,128)(2,1)S(1)} %get-tuple-element.16), channel_id=1, source_target_pairs={{48,96},{144,192},{240,288},{336,384},{432,480},{528,576},{624,672... | collective-permute-start | bytes 221192 | tf_op jit(solution)/shard_map/ppermute | solution.py:247
  29.7 2.8 %collective-permute-start = (bf16[3,8,768]{2,1,0:T(8,128)(2,1)S(1)}, bf16[3,8,768]{2,1,0:T(8,128)(2,1)S(1)}, u32[]{:S(2)}, u32[]{:S(2)}) collective-permute-start(bf16[3,8,768]{2,1,0:T(8,128)(2,1)S(1)} %get-tuple-element.13), channel_id=1, source_target_pairs={{0,1},{2,3},{4,5},{6,7},{8,9},{10,11},{12,13},{14,15},{16,17},{18,... | collective-permute-start | bytes 110600 | tf_op jit(solution)/shard_map/ppermute | solution.py:244
  32.5 4.7 %collective-permute-start.1 = (bf16[3,8,768]{2,1,0:T(8,128)(2,1)S(1)}, bf16[3,8,768]{2,1,0:T(8,128)(2,1)S(1)}, u32[]{:S(2)}, u32[]{:S(2)}) collective-permute-start(bf16[3,8,768]{2,1,0:T(8,128)(2,1)S(1)} %get-tuple-element.14), channel_id=1, source_target_pairs={{1,2},{3,4},{5,6},{7,8},{9,10},{11,12},{13,14},{15,16},{17,18},{19... | collective-permute-start | bytes 110600 | tf_op jit(solution)/shard_map/ppermute | solution.py:245
  37.2 1.1 %shard_map.78.refs_1_ = f32[3,128,768]{2,1,0:T(8,128)S(1)} custom-call(f32[3,128,768]{2,1,0:T(8,128)S(1)} %bitcast.8), custom_call_target="tpu_custom_call" | custom-call | tf_op jit(solution)/shard_map/pallas_call | solution.py:248
  38.3 0.0 all-to-all-done
  38.3 0.1 reshape.24.refs_0_
  38.4 0.0 collective-permute-done.refs_4_
  38.4 0.9 %collective-permute-done.1.refs_5_ = bf16[3,8,768]{2,1,0:T(8,128)(2,1)S(1)} collective-permute-done((bf16[3,8,768]{2,1,0:T(8,128)(2,1)S(1)}, bf16[3,8,768]{2,1,0:T(8,128)(2,1)S(1)}, u32[]{:S(2)}, u32[]{:S(2)}) %collective-permute-start.1) | collective-permute-done | bytes 36896 | tf_op jit(solution)/shard_map/ppermute | solution.py:245
  39.3 0.0 collective-permute-done.2.refs_6_
  39.3 0.0 collective-permute-done.3.refs_7_
  39.3 1.7 %shard_map.80 = (f32[3,128,768]{2,1,0:T(8,128)S(1)}, bf16[48,2,768]{2,1,0:T(2,128)(2,1)}) custom-call(bf16[96,896]{1,0:T(8,128)(2,1)S(1)} %reshape.24.refs_0_, f32[3,128,768]{2,1,0:T(8,128)S(1)} %shard_map.78.refs_1_, f32[3,128,768]{2,1,0:T(8,128)S(1)} %bitcast.9, f32[2,8,768]{2,1,0:T(8,128)S(1)} %get-tuple-element.12.refs_3_, ...), custom_call_target="tpu_custom_call", output_to_operand_aliasing={{0}: (1, {})} | custom-call | tf_op jit(solution)/shard_map/pallas_call | solution.py:255
  41.0 14.0 %all-to-all-start.1 = ((bf16[48,2,768]{2,1,0:T(2,128)(2,1)}), bf16[48,2,768]{2,1,0:T(2,128)(2,1)S(1)}, u32[]{:S(2)}, u32[]{:S(2)}) async-start(bf16[48,2,768]{2,1,0:T(2,128)(2,1)} %get-tuple-element.18), calls=%async_computation.1 | async-start | bytes 294912 | tf_op jit(solution)/shard_map/all_to_all | solution.py:262
  55.0 0.0 copy-start.1
  55.0 1.0 %copy.10 = f32[3,8,16,768]{3,2,1,0:T(8,128)} copy(f32[3,8,16,768]{3,2,1,0:T(8,128)S(1)} %bitcast.6) | data formatting | bytes 2359296
  56.0 14.1 %all-to-all-done.1 = bf16[48,2,768]{2,1,0:T(2,128)(2,1)S(1)} async-done(((bf16[48,2,768]{2,1,0:T(2,128)(2,1)}), bf16[48,2,768]{2,1,0:T(2,128)(2,1)S(1)}, u32[]{:S(2)}, u32[]{:S(2)}) %all-to-all-start.1) | async-done | bytes 147488 | tf_op jit(solution)/shard_map/all_to_all | solution.py:262
  70.1 0.1 reshape.27.back
  70.2 0.0 copy-done.1
  70.2 1.6 %shard_map.81 = f32[3,32,128]{2,1,0:T(8,128)} custom-call(bf16[96,768]{1,0:T(8,128)(2,1)S(1)} %reshape.27.back, bf16[256,128]{1,0:T(8,128)(2,1)S(1)} %get-tuple-element.19.select, bf16[32,128,256]{2,1,0:T(8,128)(2,1)S(1)} %copy-done.1), custom_call_target="tpu_custom_call" | custom-call | tf_op jit(solution)/shard_map/pallas_call | solution.py:264
Async XLA Ops:
  1.3 20.7 %copy-start = (f32[3,8,16,768]{3,2,1,0:T(8,128)S(1)}, f32[3,8,16,768]{3,2,1,0:T(8,128)}, u32[]{:S(2)}) copy-start(f32[3,8,16,768]{3,2,1,0:T(8,128)} %param.6) | copy-start | bytes 3538948
  4.3 34.0 %all-to-all-start = ((bf16[48,2,896]{2,1,0:T(2,128)(2,1)}), bf16[48,2,896]{2,1,0:T(2,128)(2,1)S(1)}, u32[]{:S(2)}, u32[]{:S(2)}) async-start(bf16[48,2,896]{2,1,0:T(2,128)(2,1)} %get-tuple-element.11), calls=%async_computation | async-start | bytes 344064 | tf_op jit(solution)/shard_map/all_to_all | solution.py:235
  22.1 17.1 %collective-permute-start.2 = (bf16[3,16,768]{2,1,0:T(8,128)(2,1)S(1)}, bf16[3,16,768]{2,1,0:T(8,128)(2,1)S(1)}, u32[]{:S(2)}, u32[]{:S(2)}) collective-permute-start(bf16[3,16,768]{2,1,0:T(8,128)(2,1)S(1)} %get-tuple-element.15), channel_id=1, source_target_pairs={{0,48},{96,144},{192,240},{288,336},{384,432},{480,528},{576,624},... | collective-permute-start | bytes 221192 | tf_op jit(solution)/shard_map/ppermute | solution.py:246
  25.2 14.1 %collective-permute-start.3 = (bf16[3,16,768]{2,1,0:T(8,128)(2,1)S(1)}, bf16[3,16,768]{2,1,0:T(8,128)(2,1)S(1)}, u32[]{:S(2)}, u32[]{:S(2)}) collective-permute-start(bf16[3,16,768]{2,1,0:T(8,128)(2,1)S(1)} %get-tuple-element.16), channel_id=1, source_target_pairs={{48,96},{144,192},{240,288},{336,384},{432,480},{528,576},{624,672... | collective-permute-start | bytes 221192 | tf_op jit(solution)/shard_map/ppermute | solution.py:247
  29.7 8.7 %collective-permute-start = (bf16[3,8,768]{2,1,0:T(8,128)(2,1)S(1)}, bf16[3,8,768]{2,1,0:T(8,128)(2,1)S(1)}, u32[]{:S(2)}, u32[]{:S(2)}) collective-permute-start(bf16[3,8,768]{2,1,0:T(8,128)(2,1)S(1)} %get-tuple-element.13), channel_id=1, source_target_pairs={{0,1},{2,3},{4,5},{6,7},{8,9},{10,11},{12,13},{14,15},{16,17},{18,... | collective-permute-start | bytes 110600 | tf_op jit(solution)/shard_map/ppermute | solution.py:244
  32.5 6.8 %collective-permute-start.1 = (bf16[3,8,768]{2,1,0:T(8,128)(2,1)S(1)}, bf16[3,8,768]{2,1,0:T(8,128)(2,1)S(1)}, u32[]{:S(2)}, u32[]{:S(2)}) collective-permute-start(bf16[3,8,768]{2,1,0:T(8,128)(2,1)S(1)} %get-tuple-element.14), channel_id=1, source_target_pairs={{1,2},{3,4},{5,6},{7,8},{9,10},{11,12},{13,14},{15,16},{17,18},{19... | collective-permute-start | bytes 110600 | tf_op jit(solution)/shard_map/ppermute | solution.py:245
  41.0 29.2 %all-to-all-start.1 = ((bf16[48,2,768]{2,1,0:T(2,128)(2,1)}), bf16[48,2,768]{2,1,0:T(2,128)(2,1)S(1)}, u32[]{:S(2)}, u32[]{:S(2)}) async-start(bf16[48,2,768]{2,1,0:T(2,128)(2,1)} %get-tuple-element.18), calls=%async_computation.1 | async-start | bytes 294912 | tf_op jit(solution)/shard_map/all_to_all | solution.py:262
  55.0 15.2 %copy-start.1 = (bf16[32,128,256]{2,1,0:T(8,128)(2,1)S(1)}, bf16[32,128,256]{2,1,0:T(8,128)(2,1)}, u32[]{:S(2)}) copy-start(bf16[32,128,256]{2,1,0:T(8,128)(2,1)} %kernels.1) | copy-start | bytes 6291460

commit v4 on v3

--- a/solution.py
+++ b/solution.py
@@ -15,6 +15,17 @@
 VMEM = pltpu.VMEM
 TRANSPOSED = (((0,), (0,)), ((), ()))
 NT = (((1,), (1,)), ((), ()))
+
+
+def ring(count):
+    half = count // 2
+    return [count - 1 - (r % 2) * half - r // 2 for r in range(count)]
+
+
+def seat(device, count):
+    half = count // 2
+    back = count - 1 - device
+    return (back % half) * 2 + back // half
 
 
 def iota(shape, axis):
@@ -62,7 +73,7 @@
     earlier = (owner == owner_row) & (there < here)
     rank = jnp.sum(earlier.astype(jnp.int32), axis=1, keepdims=True)
     live = iota((slots, 1), 0) < counts[0]
-    slot = jnp.where(live, owner * 2 + rank, -1)
+    slot = jnp.where(live, seat(owner, room // 2) * 2 + rank, -1)
     choose = (slot == iota((slots, wide), 1)).astype(F32).astype(BF16)
     grow = (iota((tall, slots), 0) // ROWS == iota((tall, slots), 1)).astype(F32).astype(BF16)
     tall_choose = dot(grow, choose)
@@ -232,7 +243,7 @@
         [VMEM((slots * ROWS, cells), F32), VMEM(kernels.shape, BF16), VMEM((comps, slots, points), BF16), VMEM((1, slots), jnp.int32), VMEM((1, slots), jnp.int32), pltpu.SemaphoreType.DMA((parts + 3,))],
         [pl.BlockSpec(memory_space=pltpu.SMEM)] + [far] * 4,
     )(counts, *[pltpu.with_memory_space_constraint(x, pltpu.HBM) for x in (kernels, forces.transpose(1, 0, 2), owners.reshape(1, slots), blocks.reshape(1, slots))])
-    got = lax.all_to_all(send, "gy", split_axis=0, concat_axis=0, tiled=True)
+    got = lax.all_to_all(send, "gy", split_axis=0, concat_axis=0, tiled=True, axis_index_groups=[ring(width_gy)])
     got = got.reshape(room, payload + LANES)
 
     z_near, z_far, y_near, y_far, lifts = call(
@@ -259,7 +270,7 @@
         [vmem] * 8,
         {1: 0},
     )(near(got), near(base), grid, near(lifts), near(y_near), near(y_far), near(z_near), near(z_far))
-    back = lax.all_to_all(picked, "gy", split_axis=0, concat_axis=0, tiled=True)
+    back = lax.all_to_all(picked, "gy", split_axis=0, concat_axis=0, tiled=True, axis_index_groups=[ring(width_gy)])
 
     (out,) = call(
         sample,

time: 72.2 us -> 68.2 us (0.945)
  starting transfers between devices: 46.8 us -> 44.6 us
  waiting for transfers between devices: 15 us -> 13.2 us
    all_to_all x2, waiting for transfers between devices: 14.1 us -> 9.64 us  [the longest x1 9.63 us: step(): lax.all_to_all(picked, 'gy', split_axis=0, concat_axis=0, tiled=True, axi...]
    ppermute x1, waiting for transfers between devices: 0.87 us -> 3.52 us  [step(): y_far = lax.ppermute(y_far, 'gy', pairs(width_gy, 1))]
    ppermute x1, starting transfers between devices: 4.71 us -> 2.06 us  [step(): y_far = lax.ppermute(y_far, 'gy', pairs(width_gy, 1))]
where the time goes in v4:
time: 68.2 us; the launch traced here: 67.8 us
  starting transfers between devices  44.6 us (65%)
  waiting for transfers between devices  13.2 us (19%)
  Pallas kernels  7.49 us (11%)
  between operations  1.41 us (2%)
  local copies, waits for them, and re-layouts  1.15 us (2%)
    all_to_all x1, starting transfers between devices, step(): lax.all_to_all(send, 'gy', split_axis=0, concat_axis=0, tiled=True, axis_...  18.7 us
    all_to_all x1, starting transfers between devices, step(): lax.all_to_all(picked, 'gy', split_axis=0, concat_axis=0, tiled=True, axi...  13.5 us
    all_to_all x1, waiting for transfers between devices, step(): lax.all_to_all(picked, 'gy', split_axis=0, concat_axis=0, tiled=True, axi...  9.63 us
    ppermute x1, starting transfers between devices, step(): z_far = lax.ppermute(z_far, 'gz', pairs(width_gz, 1))  4.75 us
    ppermute x1, waiting for transfers between devices, step(): y_far = lax.ppermute(y_far, 'gy', pairs(width_gy, 1))  3.52 us
    pallas_call x1, Pallas kernels, step(): call(lambda *refs: spread(xblocks, *refs), [S((width_gy, 2, payload + LAN...  2.97 us
    ppermute x1, starting transfers between devices, step(): y_near = lax.ppermute(y_near, 'gy', pairs(width_gy, 0))  2.88 us
    ppermute x1, starting transfers between devices, step(): z_near = lax.ppermute(z_near, 'gz', pairs(width_gz, 0))  2.75 us
  transfers between devices with their start and end apart: 6, of which 2 were waited for; matrix products, arithmetic and copies ran while one was open for 2% of the time, Pallas kernels for 2%

profile of v4, /device:TPU:27, one launch (start us, length us, event | category | flops | bytes accessed | tf_op | source)
XLA Modules:
  0.0 67.8 jit_solution(11523567869379860151)
XLA Ops:
  1.3 0.0 copy-start
  1.3 3.0 %shard_map.77 = (bf16[48,2,896]{2,1,0:T(2,128)(2,1)}, bf16[256,128]{1,0:T(8,128)(2,1)S(1)}) custom-call(s32[1]{0:T(128)S(6)} %copy.11.refs_0_, bf16[32,128,256]{2,1,0:T(8,128)(2,1)} %kernels.1, bf16[3,32,128]{2,1,0:T(8,128)(2,1)} %bitcast.11, s32[1,32]{1,0:T(1,128)} %bitcast.12, s32[1,32]{1,0:T(1,128)} %bitcast.13), custom_call_target="tpu_custom_call" | custom-call | tf_op jit(solution)/shard_map/pallas_call | solution.py:240
  4.3 18.7 %all-to-all-start = ((bf16[48,2,896]{2,1,0:T(2,128)(2,1)}), bf16[48,2,896]{2,1,0:T(2,128)(2,1)S(1)}, u32[]{:S(2)}, u32[]{:S(2)}) async-start(bf16[48,2,896]{2,1,0:T(2,128)(2,1)} %get-tuple-element.11), calls=%async_computation | async-start | bytes 344064 | tf_op jit(solution)/shard_map/all_to_all | solution.py:246
  22.9 0.0 copy-done
  22.9 0.1 shard_map.79
  23.1 2.8 %collective-permute-start.2 = (bf16[3,16,768]{2,1,0:T(8,128)(2,1)S(1)}, bf16[3,16,768]{2,1,0:T(8,128)(2,1)S(1)}, u32[]{:S(2)}, u32[]{:S(2)}) collective-permute-start(bf16[3,16,768]{2,1,0:T(8,128)(2,1)S(1)} %get-tuple-element.15), channel_id=1, source_target_pairs={{0,48},{96,144},{192,240},{288,336},{384,432},{480,528},{576,624},... | collective-permute-start | bytes 221192 | tf_op jit(solution)/shard_map/ppermute | solution.py:257
  25.8 4.8 %collective-permute-start.3 = (bf16[3,16,768]{2,1,0:T(8,128)(2,1)S(1)}, bf16[3,16,768]{2,1,0:T(8,128)(2,1)S(1)}, u32[]{:S(2)}, u32[]{:S(2)}) collective-permute-start(bf16[3,16,768]{2,1,0:T(8,128)(2,1)S(1)} %get-tuple-element.16), channel_id=1, source_target_pairs={{48,96},{144,192},{240,288},{336,384},{432,480},{528,576},{624,672... | collective-permute-start | bytes 221192 | tf_op jit(solution)/shard_map/ppermute | solution.py:258
  30.6 2.9 %collective-permute-start = (bf16[3,8,768]{2,1,0:T(8,128)(2,1)S(1)}, bf16[3,8,768]{2,1,0:T(8,128)(2,1)S(1)}, u32[]{:S(2)}, u32[]{:S(2)}) collective-permute-start(bf16[3,8,768]{2,1,0:T(8,128)(2,1)S(1)} %get-tuple-element.13), channel_id=1, source_target_pairs={{0,1},{2,3},{4,5},{6,7},{8,9},{10,11},{12,13},{14,15},{16,17},{18,... | collective-permute-start | bytes 110600 | tf_op jit(solution)/shard_map/ppermute | solution.py:255
  33.5 2.1 %collective-permute-start.1 = (bf16[3,8,768]{2,1,0:T(8,128)(2,1)S(1)}, bf16[3,8,768]{2,1,0:T(8,128)(2,1)S(1)}, u32[]{:S(2)}, u32[]{:S(2)}) collective-permute-start(bf16[3,8,768]{2,1,0:T(8,128)(2,1)S(1)} %get-tuple-element.14), channel_id=1, source_target_pairs={{1,2},{3,4},{5,6},{7,8},{9,10},{11,12},{13,14},{15,16},{17,18},{19... | collective-permute-start | bytes 110600 | tf_op jit(solution)/shard_map/ppermute | solution.py:256
  35.5 1.1 %shard_map.78.refs_1_ = f32[3,128,768]{2,1,0:T(8,128)S(1)} custom-call(f32[3,128,768]{2,1,0:T(8,128)S(1)} %bitcast.8), custom_call_target="tpu_custom_call" | custom-call | tf_op jit(solution)/shard_map/pallas_call | solution.py:259
  36.6 0.0 all-to-all-done
  36.7 0.1 reshape.24.refs_0_
  36.7 0.0 collective-permute-done.refs_4_
  36.7 3.5 %collective-permute-done.1.refs_5_ = bf16[3,8,768]{2,1,0:T(8,128)(2,1)S(1)} collective-permute-done((bf16[3,8,768]{2,1,0:T(8,128)(2,1)S(1)}, bf16[3,8,768]{2,1,0:T(8,128)(2,1)S(1)}, u32[]{:S(2)}, u32[]{:S(2)}) %collective-permute-start.1) | collective-permute-done | bytes 36896 | tf_op jit(solution)/shard_map/ppermute | solution.py:256
  40.3 0.0 collective-permute-done.2.refs_6_
  40.3 0.0 collective-permute-done.3.refs_7_
  40.3 1.7 %shard_map.80 = (f32[3,128,768]{2,1,0:T(8,128)S(1)}, bf16[48,2,768]{2,1,0:T(2,128)(2,1)}) custom-call(bf16[96,896]{1,0:T(8,128)(2,1)S(1)} %reshape.24.refs_0_, f32[3,128,768]{2,1,0:T(8,128)S(1)} %shard_map.78.refs_1_, f32[3,128,768]{2,1,0:T(8,128)S(1)} %bitcast.9, f32[2,8,768]{2,1,0:T(8,128)S(1)} %get-tuple-element.12.refs_3_, ...), custom_call_target="tpu_custom_call", output_to_operand_aliasing={{0}: (1, {})} | custom-call | tf_op jit(solution)/shard_map/pallas_call | solution.py:266
  41.9 13.5 %all-to-all-start.1 = ((bf16[48,2,768]{2,1,0:T(2,128)(2,1)}), bf16[48,2,768]{2,1,0:T(2,128)(2,1)S(1)}, u32[]{:S(2)}, u32[]{:S(2)}) async-start(bf16[48,2,768]{2,1,0:T(2,128)(2,1)} %get-tuple-element.18), calls=%async_computation.1 | async-start | bytes 294912 | tf_op jit(solution)/shard_map/all_to_all | solution.py:273
  55.5 0.0 copy-start.1
  55.5 1.0 %copy.10 = f32[3,8,16,768]{3,2,1,0:T(8,128)} copy(f32[3,8,16,768]{3,2,1,0:T(8,128)S(1)} %bitcast.6) | data formatting | bytes 2359296
  56.5 9.6 %all-to-all-done.1 = bf16[48,2,768]{2,1,0:T(2,128)(2,1)S(1)} async-done(((bf16[48,2,768]{2,1,0:T(2,128)(2,1)}), bf16[48,2,768]{2,1,0:T(2,128)(2,1)S(1)}, u32[]{:S(2)}, u32[]{:S(2)}) %all-to-all-start.1) | async-done | bytes 147488 | tf_op jit(solution)/shard_map/all_to_all | solution.py:273
  66.1 0.1 reshape.27.back
  66.2 0.0 copy-done.1
  66.2 1.6 %shard_map.81 = f32[3,32,128]{2,1,0:T(8,128)} custom-call(bf16[96,768]{1,0:T(8,128)(2,1)S(1)} %reshape.27.back, bf16[256,128]{1,0:T(8,128)(2,1)S(1)} %get-tuple-element.19.select, bf16[32,128,256]{2,1,0:T(8,128)(2,1)S(1)} %copy-done.1), custom_call_target="tpu_custom_call" | custom-call | tf_op jit(solution)/shard_map/pallas_call | solution.py:275
Async XLA Ops:
  1.3 21.6 %copy-start = (f32[3,8,16,768]{3,2,1,0:T(8,128)S(1)}, f32[3,8,16,768]{3,2,1,0:T(8,128)}, u32[]{:S(2)}) copy-start(f32[3,8,16,768]{3,2,1,0:T(8,128)} %param.6) | copy-start | bytes 3538948
  4.3 32.4 %all-to-all-start = ((bf16[48,2,896]{2,1,0:T(2,128)(2,1)}), bf16[48,2,896]{2,1,0:T(2,128)(2,1)S(1)}, u32[]{:S(2)}, u32[]{:S(2)}) async-start(bf16[48,2,896]{2,1,0:T(2,128)(2,1)} %get-tuple-element.11), calls=%async_computation | async-start | bytes 344064 | tf_op jit(solution)/shard_map/all_to_all | solution.py:246
  23.1 17.2 %collective-permute-start.2 = (bf16[3,16,768]{2,1,0:T(8,128)(2,1)S(1)}, bf16[3,16,768]{2,1,0:T(8,128)(2,1)S(1)}, u32[]{:S(2)}, u32[]{:S(2)}) collective-permute-start(bf16[3,16,768]{2,1,0:T(8,128)(2,1)S(1)} %get-tuple-element.15), channel_id=1, source_target_pairs={{0,48},{96,144},{192,240},{288,336},{384,432},{480,528},{576,624},... | collective-permute-start | bytes 221192 | tf_op jit(solution)/shard_map/ppermute | solution.py:257
  25.8 14.4 %collective-permute-start.3 = (bf16[3,16,768]{2,1,0:T(8,128)(2,1)S(1)}, bf16[3,16,768]{2,1,0:T(8,128)(2,1)S(1)}, u32[]{:S(2)}, u32[]{:S(2)}) collective-permute-start(bf16[3,16,768]{2,1,0:T(8,128)(2,1)S(1)} %get-tuple-element.16), channel_id=1, source_target_pairs={{48,96},{144,192},{240,288},{336,384},{432,480},{528,576},{624,672... | collective-permute-start | bytes 221192 | tf_op jit(solution)/shard_map/ppermute | solution.py:258
  30.6 6.1 %collective-permute-start = (bf16[3,8,768]{2,1,0:T(8,128)(2,1)S(1)}, bf16[3,8,768]{2,1,0:T(8,128)(2,1)S(1)}, u32[]{:S(2)}, u32[]{:S(2)}) collective-permute-start(bf16[3,8,768]{2,1,0:T(8,128)(2,1)S(1)} %get-tuple-element.13), channel_id=1, source_target_pairs={{0,1},{2,3},{4,5},{6,7},{8,9},{10,11},{12,13},{14,15},{16,17},{18,... | collective-permute-start | bytes 110600 | tf_op jit(solution)/shard_map/ppermute | solution.py:255
  33.5 6.8 %collective-permute-start.1 = (bf16[3,8,768]{2,1,0:T(8,128)(2,1)S(1)}, bf16[3,8,768]{2,1,0:T(8,128)(2,1)S(1)}, u32[]{:S(2)}, u32[]{:S(2)}) collective-permute-start(bf16[3,8,768]{2,1,0:T(8,128)(2,1)S(1)} %get-tuple-element.14), channel_id=1, source_target_pairs={{1,2},{3,4},{5,6},{7,8},{9,10},{11,12},{13,14},{15,16},{17,18},{19... | collective-permute-start | bytes 110600 | tf_op jit(solution)/shard_map/ppermute | solution.py:256
  41.9 24.2 %all-to-all-start.1 = ((bf16[48,2,768]{2,1,0:T(2,128)(2,1)}), bf16[48,2,768]{2,1,0:T(2,128)(2,1)S(1)}, u32[]{:S(2)}, u32[]{:S(2)}) async-start(bf16[48,2,768]{2,1,0:T(2,128)(2,1)} %get-tuple-element.18), calls=%async_computation.1 | async-start | bytes 294912 | tf_op jit(solution)/shard_map/all_to_all | solution.py:273
  55.5 10.7 %copy-start.1 = (bf16[32,128,256]{2,1,0:T(8,128)(2,1)S(1)}, bf16[32,128,256]{2,1,0:T(8,128)(2,1)}, u32[]{:S(2)}) copy-start(bf16[32,128,256]{2,1,0:T(8,128)(2,1)} %kernels.1) | copy-start | bytes 6291460

commit v5 on v4

--- a/solution.py
+++ b/solution.py
@@ -43,7 +43,14 @@
 
 
 def spread(xblocks, counts, *refs):
-    sources, (send, select, product, kernels), small, arrived = refs[:4], refs[4:8], refs[8:11], refs[11]
+    sources, (outbox, select, product, kernels), small, arrived, send, sent = refs[:4], refs[4:8], refs[8:11], refs[11], refs[12], refs[13]
+    leaving = []
+
+    def leave(start, size):
+        span = pl.ds(start, size)
+        leaving.append(pltpu.make_async_copy(send.at[:, :, span], outbox.at[:, :, span], sent.at[len(leaving)]))
+        leaving[-1].start()
+
     forces, owners, blocks = small
     slots = kernels.shape[0]
     parts = arrived.shape[0] - len(small)
@@ -57,7 +64,7 @@
     for i in range(parts):
         span = pl.ds(i * each, each)
         copies.append(pltpu.make_async_copy(source.at[span], kernels.at[span], arrived.at[i]))
-        copies[-1].start()
+        copies[-1].start(priority=i % 2)
     comps = forces.shape[0]
     cells = kernels.shape[2]
     room = send.shape[0] * send.shape[1]
@@ -80,6 +87,11 @@
     select[...] = tall_choose.astype(BF16)
     grow_t = (iota((slots, tall), 1) // ROWS == iota((slots, tall), 0)).astype(F32).astype(BF16)
     wide_choose = dot(choose, grow_t, TRANSPOSED)
+    where = iota((slots, LANES), 1)
+    words = jnp.where(where == 0, block // xblocks, jnp.where(where == 1, block % xblocks, jnp.where(where == 2, 1, 0)))
+    tags = dot(choose, words.astype(F32).astype(BF16), TRANSPOSED)
+    send[:, :, comps * cells:] = tags[:room].reshape(room // 2, 2, LANES).astype(BF16)
+    leave(comps * cells, LANES)
     flat = forces[...].reshape(comps * slots, forces.shape[2])
     r = iota((tall, comps * slots), 0)
     s = iota((tall, comps * slots), 1)
@@ -95,10 +107,9 @@
     for c in range(comps):
         pick = jnp.where(lane == c, wide_choose, 0.0).astype(BF16)
         send[:, :, c * cells:(c + 1) * cells] = dot(pick, made)[:room].reshape(room // 2, 2, cells).astype(BF16)
-    where = iota((slots, LANES), 1)
-    words = jnp.where(where == 0, block // xblocks, jnp.where(where == 1, block % xblocks, jnp.where(where == 2, 1, 0)))
-    tags = dot(choose, words.astype(F32).astype(BF16), TRANSPOSED)
-    send[:, :, comps * cells:] = tags[:room].reshape(room // 2, 2, LANES).astype(BF16)
+        leave(c * cells, cells)
+    for copy in leaving:
+        copy.wait()
 
 
 def even(axis):
@@ -143,7 +154,7 @@
             base[c, span, :] = v + time_step * (viscosity * lap - adv)
 
 
-def exchange(cells, planes, got, base, velocity, lifts, y_near, y_far, z_near, z_far, fresh, send):
+def exchange(cells, planes, got, base, velocity, lifts, y_near, y_far, z_near, z_far, fresh, target, send, sent):
     comps, height, xcells = base.shape
     rows = height // planes
     room = got.shape[0]
@@ -161,6 +172,7 @@
     turned = [jnp.concatenate([p, edges], axis=0).T.astype(BF16) for p in picks]
     lift = velocity[comps - 1, :rows, :] * (0.5 * time_step) + viscosity * time_step
     sink = viscosity * time_step - velocity[comps - 1, height - rows:, :] * (0.5 * time_step)
+    leaving = []
     for c in range(comps):
         one, two = z_near[c].astype(F32), z_far[c].astype(F32)
         low = jnp.where(z_even, two, one) * lift
@@ -178,7 +190,12 @@
             fresh[c, :, lanes] = new
             part = dot(narrow[b], new.astype(BF16))
             total = part if total is None else total + part
-        send[:, :, c * cells:(c + 1) * cells] = total.reshape(send.shape[0], 2, cells).astype(BF16)
+        span = pl.ds(c * cells, cells)
+        send[:, :, span] = total.reshape(send.shape[0], 2, cells).astype(BF16)
+        leaving.append(pltpu.make_async_copy(send.at[:, :, span], target.at[:, :, span], sent.at[c]))
+        leaving[-1].start()
+    for copy in leaving:
+        copy.wait()
 
 
 def sample(back, select, kernels, out, result):
@@ -200,12 +217,12 @@
         out[c] = result[pl.ds(c, slots, stride=ROWS), :]
 
 
-def call(body, outs, scratch, ins, aliases={}):
+def call(body, outs, scratch, ins, aliases={}, places=None):
     return pl.pallas_call(
         body,
         out_shape=outs,
         in_specs=ins,
-        out_specs=[pl.BlockSpec(memory_space=VMEM)] * len(outs),
+        out_specs=places or [pl.BlockSpec(memory_space=VMEM)] * len(outs),
         scratch_shapes=scratch,
         input_output_aliases=aliases,
         compiler_params=pltpu.CompilerParams(vmem_limit_bytes=16 * 1024 * 1024),
@@ -239,9 +256,10 @@
 
     send, select = call(
         lambda *refs: spread(xblocks, *refs),
-        [S((width_gy, 2, payload + LANES), BF16), S((slots * ROWS, wide), BF16)],
-        [VMEM((slots * ROWS, cells), F32), VMEM(kernels.shape, BF16), VMEM((comps, slots, points), BF16), VMEM((1, slots), jnp.int32), VMEM((1, slots), jnp.int32), pltpu.SemaphoreType.DMA((parts + 3,))],
+        [jax.ShapeDtypeStruct((width_gy, 2, payload + LANES), BF16), S((slots * ROWS, wide), BF16)],
+        [VMEM((slots * ROWS, cells), F32), VMEM(kernels.shape, BF16), VMEM((comps, slots, points), BF16), VMEM((1, slots), jnp.int32), VMEM((1, slots), jnp.int32), pltpu.SemaphoreType.DMA((parts + 3,)), VMEM((width_gy, 2, payload + LANES), BF16), pltpu.SemaphoreType.DMA((comps + 1,))],
         [pl.BlockSpec(memory_space=pltpu.SMEM)] + [far] * 4,
+        places=[far, vmem],
     )(counts, *[pltpu.with_memory_space_constraint(x, pltpu.HBM) for x in (kernels, forces.transpose(1, 0, 2), owners.reshape(1, slots), blocks.reshape(1, slots))])
     got = lax.all_to_all(send, "gy", split_axis=0, concat_axis=0, tiled=True, axis_index_groups=[ring(width_gy)])
     got = got.reshape(room, payload + LANES)
@@ -265,10 +283,11 @@
 
     fresh, picked = call(
         lambda *refs: exchange(cells, planes, *refs),
-        [S(grid.shape, F32), S((width_gy, 2, payload), BF16)],
-        [],
+        [S(grid.shape, F32), jax.ShapeDtypeStruct((width_gy, 2, payload), BF16)],
+        [VMEM((width_gy, 2, payload), BF16), pltpu.SemaphoreType.DMA((comps,))],
         [vmem] * 8,
         {1: 0},
+        [vmem, far],
     )(near(got), near(base), grid, near(lifts), near(y_near), near(y_far), near(z_near), near(z_far))
     back = lax.all_to_all(picked, "gy", split_axis=0, concat_axis=0, tiled=True, axis_index_groups=[ring(width_gy)])
 

time: 68.2 us -> 68.2 us (level)
  no operation moved by 1% of the time
where the time goes in v5:
time: 68.2 us; the launch traced here: 67.9 us
  starting transfers between devices  44.6 us (65%)
  waiting for transfers between devices  13.2 us (19%)
  Pallas kernels  7.53 us (11%)
  between operations  1.41 us (2%)
  local copies, waits for them, and re-layouts  1.15 us (2%)
    all_to_all x1, starting transfers between devices, step(): lax.all_to_all(send, 'gy', split_axis=0, concat_axis=0, tiled=True, axis_...  18.7 us
    all_to_all x1, starting transfers between devices, step(): lax.all_to_all(picked, 'gy', split_axis=0, concat_axis=0, tiled=True, axi...  13.5 us
    all_to_all x1, waiting for transfers between devices, step(): lax.all_to_all(picked, 'gy', split_axis=0, concat_axis=0, tiled=True, axi...  9.63 us
    ppermute x1, starting transfers between devices, step(): z_far = lax.ppermute(z_far, 'gz', pairs(width_gz, 1))  4.75 us
    ppermute x1, waiting for transfers between devices, step(): y_far = lax.ppermute(y_far, 'gy', pairs(width_gy, 1))  3.52 us
    pallas_call x1, Pallas kernels, step(): call(lambda *refs: spread(xblocks, *refs), [jax.ShapeDtypeStruct((width_g...  3.01 us
    ppermute x1, starting transfers between devices, step(): y_near = lax.ppermute(y_near, 'gy', pairs(width_gy, 0))  2.88 us
    ppermute x1, starting transfers between devices, step(): z_near = lax.ppermute(z_near, 'gz', pairs(width_gz, 0))  2.75 us
  transfers between devices with their start and end apart: 6, of which 2 were waited for; matrix products, arithmetic and copies ran while one was open for 2% of the time, Pallas kernels for 2%

profile of v5, /device:TPU:27, one launch (start us, length us, event | category | flops | bytes accessed | tf_op | source)
XLA Modules:
  0.0 67.9 jit_solution(9951269486987980)
XLA Ops:
  1.3 0.0 copy-start
  1.3 3.0 %shard_map.77 = (bf16[48,2,896]{2,1,0:T(2,128)(2,1)}, bf16[256,128]{1,0:T(8,128)(2,1)S(1)}) custom-call(s32[1]{0:T(128)S(6)} %copy.11.refs_0_, bf16[32,128,256]{2,1,0:T(8,128)(2,1)} %kernels.1, bf16[3,32,128]{2,1,0:T(8,128)(2,1)} %bitcast.11, s32[1,32]{1,0:T(1,128)} %bitcast.12, s32[1,32]{1,0:T(1,128)} %bitcast.13), custom_call_target="tpu_custom_call" | custom-call | tf_op jit(solution)/shard_map/pallas_call | solution.py:257
  4.3 18.7 %all-to-all-start = ((bf16[48,2,896]{2,1,0:T(2,128)(2,1)}), bf16[48,2,896]{2,1,0:T(2,128)(2,1)S(1)}, u32[]{:S(2)}, u32[]{:S(2)}) async-start(bf16[48,2,896]{2,1,0:T(2,128)(2,1)} %get-tuple-element.11), calls=%async_computation | async-start | bytes 344064 | tf_op jit(solution)/shard_map/all_to_all | solution.py:264
  23.0 0.0 copy-done
  23.0 0.1 shard_map.79
  23.1 2.8 %collective-permute-start.2 = (bf16[3,16,768]{2,1,0:T(8,128)(2,1)S(1)}, bf16[3,16,768]{2,1,0:T(8,128)(2,1)S(1)}, u32[]{:S(2)}, u32[]{:S(2)}) collective-permute-start(bf16[3,16,768]{2,1,0:T(8,128)(2,1)S(1)} %get-tuple-element.15), channel_id=1, source_target_pairs={{0,48},{96,144},{192,240},{288,336},{384,432},{480,528},{576,624},... | collective-permute-start | bytes 221192 | tf_op jit(solution)/shard_map/ppermute | solution.py:275
  25.9 4.8 %collective-permute-start.3 = (bf16[3,16,768]{2,1,0:T(8,128)(2,1)S(1)}, bf16[3,16,768]{2,1,0:T(8,128)(2,1)S(1)}, u32[]{:S(2)}, u32[]{:S(2)}) collective-permute-start(bf16[3,16,768]{2,1,0:T(8,128)(2,1)S(1)} %get-tuple-element.16), channel_id=1, source_target_pairs={{48,96},{144,192},{240,288},{336,384},{432,480},{528,576},{624,672... | collective-permute-start | bytes 221192 | tf_op jit(solution)/shard_map/ppermute | solution.py:276
  30.6 2.9 %collective-permute-start = (bf16[3,8,768]{2,1,0:T(8,128)(2,1)S(1)}, bf16[3,8,768]{2,1,0:T(8,128)(2,1)S(1)}, u32[]{:S(2)}, u32[]{:S(2)}) collective-permute-start(bf16[3,8,768]{2,1,0:T(8,128)(2,1)S(1)} %get-tuple-element.13), channel_id=1, source_target_pairs={{0,1},{2,3},{4,5},{6,7},{8,9},{10,11},{12,13},{14,15},{16,17},{18,... | collective-permute-start | bytes 110600 | tf_op jit(solution)/shard_map/ppermute | solution.py:273
  33.5 2.1 %collective-permute-start.1 = (bf16[3,8,768]{2,1,0:T(8,128)(2,1)S(1)}, bf16[3,8,768]{2,1,0:T(8,128)(2,1)S(1)}, u32[]{:S(2)}, u32[]{:S(2)}) collective-permute-start(bf16[3,8,768]{2,1,0:T(8,128)(2,1)S(1)} %get-tuple-element.14), channel_id=1, source_target_pairs={{1,2},{3,4},{5,6},{7,8},{9,10},{11,12},{13,14},{15,16},{17,18},{19... | collective-permute-start | bytes 110600 | tf_op jit(solution)/shard_map/ppermute | solution.py:274
  35.6 1.1 %shard_map.78.refs_1_ = f32[3,128,768]{2,1,0:T(8,128)S(1)} custom-call(f32[3,128,768]{2,1,0:T(8,128)S(1)} %bitcast.8), custom_call_target="tpu_custom_call" | custom-call | tf_op jit(solution)/shard_map/pallas_call | solution.py:277
  36.7 0.0 all-to-all-done
  36.7 0.1 reshape.24.refs_0_
  36.8 0.0 collective-permute-done.refs_4_
  36.8 3.5 %collective-permute-done.1.refs_5_ = bf16[3,8,768]{2,1,0:T(8,128)(2,1)S(1)} collective-permute-done((bf16[3,8,768]{2,1,0:T(8,128)(2,1)S(1)}, bf16[3,8,768]{2,1,0:T(8,128)(2,1)S(1)}, u32[]{:S(2)}, u32[]{:S(2)}) %collective-permute-start.1) | collective-permute-done | bytes 36896 | tf_op jit(solution)/shard_map/ppermute | solution.py:274
  40.3 0.0 collective-permute-done.2.refs_6_
  40.3 0.0 collective-permute-done.3.refs_7_
  40.3 1.7 %shard_map.80 = (f32[3,128,768]{2,1,0:T(8,128)S(1)}, bf16[48,2,768]{2,1,0:T(2,128)(2,1)}) custom-call(bf16[96,896]{1,0:T(8,128)(2,1)S(1)} %reshape.24.refs_0_, f32[3,128,768]{2,1,0:T(8,128)S(1)} %shard_map.78.refs_1_, f32[3,128,768]{2,1,0:T(8,128)S(1)} %bitcast.9, f32[2,8,768]{2,1,0:T(8,128)S(1)} %get-tuple-element.12.refs_3_, ...), custom_call_target="tpu_custom_call", output_to_operand_aliasing={{0}: (1, {})} | custom-call | tf_op jit(solution)/shard_map/pallas_call | solution.py:284
  42.0 13.5 %all-to-all-start.1 = ((bf16[48,2,768]{2,1,0:T(2,128)(2,1)}), bf16[48,2,768]{2,1,0:T(2,128)(2,1)S(1)}, u32[]{:S(2)}, u32[]{:S(2)}) async-start(bf16[48,2,768]{2,1,0:T(2,128)(2,1)} %get-tuple-element.18), calls=%async_computation.1 | async-start | bytes 294912 | tf_op jit(solution)/shard_map/all_to_all | solution.py:292
  55.5 0.0 copy-start.1
  55.5 1.0 %copy.10 = f32[3,8,16,768]{3,2,1,0:T(8,128)} copy(f32[3,8,16,768]{3,2,1,0:T(8,128)S(1)} %bitcast.6) | data formatting | bytes 2359296
  56.6 9.6 %all-to-all-done.1 = bf16[48,2,768]{2,1,0:T(2,128)(2,1)S(1)} async-done(((bf16[48,2,768]{2,1,0:T(2,128)(2,1)}), bf16[48,2,768]{2,1,0:T(2,128)(2,1)S(1)}, u32[]{:S(2)}, u32[]{:S(2)}) %all-to-all-start.1) | async-done | bytes 147488 | tf_op jit(solution)/shard_map/all_to_all | solution.py:292
  66.2 0.1 reshape.27.back
  66.3 0.0 copy-done.1
  66.3 1.6 %shard_map.81 = f32[3,32,128]{2,1,0:T(8,128)} custom-call(bf16[96,768]{1,0:T(8,128)(2,1)S(1)} %reshape.27.back, bf16[256,128]{1,0:T(8,128)(2,1)S(1)} %get-tuple-element.19.select, bf16[32,128,256]{2,1,0:T(8,128)(2,1)S(1)} %copy-done.1), custom_call_target="tpu_custom_call" | custom-call | tf_op jit(solution)/shard_map/pallas_call | solution.py:294
Async XLA Ops:
  1.3 21.7 %copy-start = (f32[3,8,16,768]{3,2,1,0:T(8,128)S(1)}, f32[3,8,16,768]{3,2,1,0:T(8,128)}, u32[]{:S(2)}) copy-start(f32[3,8,16,768]{3,2,1,0:T(8,128)} %param.6) | copy-start | bytes 3538948
  4.3 32.4 %all-to-all-start = ((bf16[48,2,896]{2,1,0:T(2,128)(2,1)}), bf16[48,2,896]{2,1,0:T(2,128)(2,1)S(1)}, u32[]{:S(2)}, u32[]{:S(2)}) async-start(bf16[48,2,896]{2,1,0:T(2,128)(2,1)} %get-tuple-element.11), calls=%async_computation | async-start | bytes 344064 | tf_op jit(solution)/shard_map/all_to_all | solution.py:264
  23.1 17.2 %collective-permute-start.2 = (bf16[3,16,768]{2,1,0:T(8,128)(2,1)S(1)}, bf16[3,16,768]{2,1,0:T(8,128)(2,1)S(1)}, u32[]{:S(2)}, u32[]{:S(2)}) collective-permute-start(bf16[3,16,768]{2,1,0:T(8,128)(2,1)S(1)} %get-tuple-element.15), channel_id=1, source_target_pairs={{0,48},{96,144},{192,240},{288,336},{384,432},{480,528},{576,624},... | collective-permute-start | bytes 221192 | tf_op jit(solution)/shard_map/ppermute | solution.py:275
  25.9 14.4 %collective-permute-start.3 = (bf16[3,16,768]{2,1,0:T(8,128)(2,1)S(1)}, bf16[3,16,768]{2,1,0:T(8,128)(2,1)S(1)}, u32[]{:S(2)}, u32[]{:S(2)}) collective-permute-start(bf16[3,16,768]{2,1,0:T(8,128)(2,1)S(1)} %get-tuple-element.16), channel_id=1, source_target_pairs={{48,96},{144,192},{240,288},{336,384},{432,480},{528,576},{624,672... | collective-permute-start | bytes 221192 | tf_op jit(solution)/shard_map/ppermute | solution.py:276
  30.6 6.1 %collective-permute-start = (bf16[3,8,768]{2,1,0:T(8,128)(2,1)S(1)}, bf16[3,8,768]{2,1,0:T(8,128)(2,1)S(1)}, u32[]{:S(2)}, u32[]{:S(2)}) collective-permute-start(bf16[3,8,768]{2,1,0:T(8,128)(2,1)S(1)} %get-tuple-element.13), channel_id=1, source_target_pairs={{0,1},{2,3},{4,5},{6,7},{8,9},{10,11},{12,13},{14,15},{16,17},{18,... | collective-permute-start | bytes 110600 | tf_op jit(solution)/shard_map/ppermute | solution.py:273
  33.5 6.8 %collective-permute-start.1 = (bf16[3,8,768]{2,1,0:T(8,128)(2,1)S(1)}, bf16[3,8,768]{2,1,0:T(8,128)(2,1)S(1)}, u32[]{:S(2)}, u32[]{:S(2)}) collective-permute-start(bf16[3,8,768]{2,1,0:T(8,128)(2,1)S(1)} %get-tuple-element.14), channel_id=1, source_target_pairs={{1,2},{3,4},{5,6},{7,8},{9,10},{11,12},{13,14},{15,16},{17,18},{19... | collective-permute-start | bytes 110600 | tf_op jit(solution)/shard_map/ppermute | solution.py:274
  42.0 24.2 %all-to-all-start.1 = ((bf16[48,2,768]{2,1,0:T(2,128)(2,1)}), bf16[48,2,768]{2,1,0:T(2,128)(2,1)S(1)}, u32[]{:S(2)}, u32[]{:S(2)}) async-start(bf16[48,2,768]{2,1,0:T(2,128)(2,1)} %get-tuple-element.18), calls=%async_computation.1 | async-start | bytes 294912 | tf_op jit(solution)/shard_map/all_to_all | solution.py:292
  55.5 10.7 %copy-start.1 = (bf16[32,128,256]{2,1,0:T(8,128)(2,1)S(1)}, bf16[32,128,256]{2,1,0:T(8,128)(2,1)}, u32[]{:S(2)}) copy-start(bf16[32,128,256]{2,1,0:T(8,128)(2,1)} %kernels.1) | copy-start | bytes 6291460
